TPU v7x, 256 devices: a whole 4x4x8 slice. The times are simulated.
256 devices in a mesh: row: 8 (over y, z_lo), col: 4 (over x), band: 8 (over z_hi, core).
Axes of the slice: x: 4, y: 4, z: 8 (z_hi: 4, z_lo: 2; z = z_hi * 2 + z_lo), core: 2. Of those that a mesh axis runs over, the one named last changes fastest.
Arguments:
- noisy: float32 [224, 128, 4096], P('band', 'row', 'col'), may hold values from -4 to 4
- weight_map: float32 [128, 4096], P('row', 'col'), may hold values from 1.5 to 12
Outputs:
- denoised: float32 [224, 128, 4096], P('band', 'row', 'col')
All inputs are finite; a program needn't handle non-finite values.
Results may differ from a plain program's by a relative error of at most 0.0001.
Values sent between devices are 32-bit elements; how exact they have to be, the bound alone decides.
No kernel may reach another device: no remote copies, remote signals or barrier semaphores. Data moves between devices by JAX's collectives and lax.ppermute only.
A program may use at most 64 MiB of HBM per device.

v0:
```python
import jax
import jax.numpy as jnp
from jax import lax
from jax.experimental import pallas as pl
from jax.experimental.pallas import tpu as pltpu
from jax.sharding import PartitionSpec as P


ITERS = 4
M = ITERS
LANES = 128
SIGMA = 0.35
TAU = 0.35


F32 = jnp.float32
U0, QX0, QY0, NE0 = range(4)
VM = pl.BlockSpec(memory_space=pltpu.VMEM)
SM = pl.BlockSpec(memory_space=pltpu.SMEM)
HB = pl.BlockSpec(memory_space=pltpu.HBM)
PARAMS = pltpu.CompilerParams(vmem_limit_bytes=8 * 1024 * 1024)


def call(body, outs, ins, n_smem=0, aliases=None, scratch=(), flops=0, hbm_in=(), hbm_out=()):
    in_specs = [SM] * n_smem + [VM] * (len(ins) - n_smem)
    return pl.pallas_call(
        body,
        out_shape=[(pltpu.HBM if i in hbm_out else pltpu.VMEM)(s, F32) for i, s in enumerate(outs)],
        in_specs=[HB if i in hbm_in else spec for i, spec in enumerate(in_specs)],
        out_specs=[HB if i in hbm_out else VM for i in range(len(outs))],
        scratch_shapes=list(scratch),
        input_output_aliases=aliases or {},
        compiler_params=PARAMS,
        cost_estimate=pl.CostEstimate(flops=flops, bytes_accessed=0, transcendentals=0),
    )(*ins)


def here():
    band = lax.axis_index("band")
    core = lax.rem(band, 2)
    return core, core ^ lax.rem(lax.div(band, 2), 2), lax.rem(lax.axis_index("row"), 2)


def lane_iota(shape):
    return lax.broadcasted_iota(jnp.int32, shape, len(shape) - 1)


class Sizes:
    def __init__(self, bands, rows, cols):
        self.b = bands
        self.nb = 2 * bands
        self.bt = self.nb // 8
        self.r = rows
        self.c = cols // 2
        self.er = rows + 2 * M
        self.ec = self.c + LANES
        self.full = self.b // 8 * 8
        self.rest = self.b - self.full
        self.ft = self.full // 8
        self.rg = rows // 8
        self.lt = self.c // LANES
        self.block = (self.rg, self.lt, self.b, 8, LANES)


def pack_lanes(tiles, first, width):
    per = LANES // width
    lane = lane_iota((8, LANES))
    out = []
    for v in range(0, len(tiles), per):
        acc = None
        for p, tile in enumerate(tiles[v : v + per]):
            moved = pltpu.roll(tile, (p * width - first) % LANES, axis=1)
            acc = moved if acc is None else jnp.where(lane // width == p, moved, acc)
        out.append(acc)
    return out


def flat_rows(ref, *at):
    tile = ref.at[at]
    return tile.reshape(tile.shape[0] * 8, LANES)


def half_copies(z, half, array, block, sem, group=None, out=False):
    copies = []
    for g in range(z.rg) if group is None else (None,):
        rows = pl.ds(8 * g, 8) if group is None else pl.ds(pl.multiple_of(group * 8, 8), 8)
        for t in range(z.lt):
            lanes = pl.ds(pl.multiple_of(half * z.c + t * LANES, LANES), LANES)
            ends = [array.at[:, rows, lanes], block.at[t] if group is not None else block.at[g, t]]
            copies.append(pltpu.make_async_copy(*(ends[::-1] if out else ends), sem.at[(g or 0) * z.lt + t]))
    return copies


def split(z, facing_b, place, noisy, edge, *refs):
    weights, (keep, send, msg_keep, msg_send), more = refs[0], refs[facing_b : facing_b + 4], refs[facing_b + 4 :]
    sem_k, sem_s = more[facing_b : facing_b + 2]
    half, odd = place[1], place[2]
    group = odd if facing_b else 1 - odd
    copies = half_copies(z, half, noisy, keep, sem_k, group) + half_copies(z, 1 - half, noisy, send, sem_s, group)
    if facing_b:
        lanes = pl.ds(pl.multiple_of(half * z.c, LANES), z.c)
        copies.append(pltpu.make_async_copy(weights.at[:, lanes], more[0], more[3]))
    for c in copies:
        c.start()
    for c in copies:
        c.wait()

    def rows(block, first, msg):
        for i in range(M):
            q = first + i
            for t in range(z.lt):
                run = flat_rows(block, t)
                lanes = slice(t * LANES, (t + 1) * LANES)
                for bt in range(z.ft):
                    msg[z.ft * i + bt, :, lanes] = run[pl.ds(64 * bt + q, 8, stride=8), :]
                at = z.rest * (i % 2)
                msg[z.ft * M + i // 2, at : at + z.rest, lanes] = run[pl.ds(8 * z.full + q, z.rest, stride=8), :]

    @pl.when(group == 0)
    def _():
        rows(keep, 0, msg_keep)
        rows(send, 0, msg_send)

    @pl.when(group == 1)
    def _():
        rows(keep, 8 - M, msg_keep)
        rows(send, 8 - M, msg_send)


def assemble(z, place, keep_a, send_a, keep_b, send_b, w, edge, ne, col_l, col_r):
    core, odd = place[0], place[2]
    q4 = z.rest
    for keep, recv, group in ((keep_a, send_a, 1 - odd), (keep_b, send_b, odd)):
        for q in range(8):
            e = NE0 + M + 8 * group + q
            for t in range(z.lt):
                lanes = slice(t * LANES, (t + 1) * LANES)
                mine, other = flat_rows(keep, t), flat_rows(recv, t)
                for bt in range(z.ft):
                    ne[e, core * z.ft + bt, :, lanes] = mine[pl.ds(64 * bt + q, 8, stride=8), :]
                    ne[e, (1 - core) * z.ft + bt, :, lanes] = other[pl.ds(64 * bt + q, 8, stride=8), :]
                a = mine[pl.ds(8 * z.full + q, q4, stride=8), :]
                b = other[pl.ds(8 * z.full + q, q4, stride=8), :]
                ne[e, 2 * z.ft, 0:q4, lanes] = jnp.where(core == 0, a, b)
                ne[e, 2 * z.ft, q4:8, lanes] = jnp.where(core == 0, b, a)
    last = slice(z.c - LANES, z.c)
    left = [ne[NE0 + M + r, t, :, 0:LANES] for r in range(z.r) for t in range(z.bt)]
    left += [w[8 * t : 8 * t + 8, 0:LANES] for t in range(z.r // 8)]
    right = [ne[NE0 + M + r, t, :, last] for r in range(z.r) for t in range(z.bt)]
    right += [w[8 * t : 8 * t + 8, last] for t in range(z.r // 8)]
    for v, tile in enumerate(pack_lanes(left, 0, M)):
        col_l[v] = tile
    for v, tile in enumerate(pack_lanes(right, LANES - M, M)):
        col_r[v] = tile


def frame_cols(z, place, ne_in, w, edge, from_r, from_l, ne, wx, qx, qy, sums, cor_a, cor_b, acc):
    lane = lane_iota((8, LANES))
    per = LANES // M
    units = z.r * z.bt + z.r // 8
    tiles = []
    for k in range(units):
        v, p = divmod(k, per)
        hi = pltpu.roll(from_r[v], (-p * M) % LANES, axis=1)
        lo = pltpu.roll(from_l[v], (LANES - M - p * M) % LANES, axis=1)
        tiles.append(jnp.where(lane < M, hi, jnp.where(lane >= LANES - M, lo, 0.0)))
    for r in range(z.r):
        for t in range(z.bt):
            ne[NE0 + M + r, t, :, z.c : z.ec] = tiles[r * z.bt + t]
    wx[0:M, :] = jnp.zeros((M, z.ec), F32)
    wx[M + z.r : z.er, :] = jnp.zeros((M, z.ec), F32)
    wx[M : M + z.r, 0 : z.c] = w[...]
    for t in range(z.r // 8):
        wx[M + 8 * t : M + 8 * t + 8, z.c : z.ec] = tiles[z.r * z.bt + t]
    up = tiles[: M * z.bt] + [tiles[z.r * z.bt]]
    down = tiles[(z.r - M) * z.bt : z.r * z.bt] + [tiles[units - 1]]
    up, down = (pack_lanes(x, LANES - M, 2 * M) for x in (up, down))
    lanes = [slice(t * LANES, (t + 1) * LANES) for t in range(z.lt)]
    up += [w[0:8, x] for x in lanes]
    down += [w[z.r - 8 : z.r, x] for x in lanes]
    odd = place[2]
    for v, (u, d) in enumerate(zip(up, down)):
        cor_a[v] = jnp.where(odd == 0, d, u)
        cor_b[v] = jnp.where(odd == 0, u, d)
    sums[...] = jnp.zeros_like(sums)
    first_q(z, ne, edge, [(M, M + z.r - 1)], qx, qy, acc, sums)


def first_q(z, ne, edge, runs, qx, qy, acc, sums):
    across, along = masks(z, edge)
    acc[...] = jnp.zeros_like(acc)

    def band_tile(t, _):
        for lo, hi in runs:
            here = ne[NE0 + lo, t]
            for e in range(lo, hi):
                below_row = ne[NE0 + e + 1, t]
                gx = across(e, below_row - here)
                gy = along(pltpu.roll(here, z.ec - 1, axis=1) - here)
                qx[QX0 + e, t] = gx
                qy[QY0 + e, t] = gy
                acc[e] = acc[e] + (gx * gx + gy * gy)
                here = below_row
        return 0

    lax.fori_loop(0, z.bt, band_tile, 0)
    for lo, hi in runs:
        for e in range(lo, hi):
            sums[e : e + 1, :] = jnp.sum(acc[e], axis=0, keepdims=True)


def masks(z, edge):
    rows = {M - 1: edge[0:1, :], M + z.r - 1: edge[1:2, :]}
    cut = z.c - LANES
    tail = jnp.broadcast_to(edge[2:3, cut : z.ec], (8, z.ec - cut))

    def across(e, d):
        return d * rows[e] if e in rows else d

    def along(d):
        return jnp.concatenate([d[:, 0:cut], d[:, cut : z.ec] * tail], axis=1)

    return across, along


def message_rows(z, k):
    lo, hi = k, z.er - 1 - k
    return lo, hi - lo + (hi - lo) % 2


def message_shape(z, k):
    return (message_rows(z, k)[1] * (z.c // LANES) + 8, LANES)


def write_message(z, k, acc, sums, msg):
    lo, hi = k, z.er - 1 - k
    sums[...] = jnp.zeros_like(sums)
    for e in range(lo, hi):
        sums[e : e + 1, :] = jnp.sum(acc[e], axis=0, keepdims=True)
    pack_message(z, k, sums, msg)


def pack_message(z, k, sums, msg):
    first, n = message_rows(z, k)
    for t in range(z.c // LANES):
        msg[t * n : (t + 1) * n, :] = sums[first : first + n, t * LANES : (t + 1) * LANES]
    halo = [sums[8 * g : 8 * g + 8, z.c : z.ec] for g in range(z.er // 8)]
    msg[n * (z.c // LANES) :, :] = pack_lanes(halo, LANES - M, 2 * M)[0]


def read_scale(z, k, msg_a, msg_b, wx, sums, scale):
    lo, hi = k, z.er - 1 - k
    first, n = message_rows(z, k)
    lane = lane_iota((8, LANES))
    sums[...] = jnp.zeros_like(sums)
    for t in range(z.c // LANES):
        part = slice(t * n, (t + 1) * n)
        sums[first : first + n, t * LANES : (t + 1) * LANES] = msg_a[part, :] + msg_b[part, :]
    packed = msg_a[n * (z.c // LANES) :, :] + msg_b[n * (z.c // LANES) :, :]
    for g in range(z.er // 8):
        got = pltpu.roll(packed, (LANES - M - g * 2 * M) % LANES, axis=1)
        sums[8 * g : 8 * g + 8, z.c : z.ec] = jnp.where((lane < M) | (lane >= LANES - M), got, 0.0)
    w = wx[...]
    sums[...] = w / jnp.maximum(w, jnp.sqrt(1.0 + (SIGMA * SIGMA) * sums[...]))
    for e in range(lo, hi):
        scale[e] = jnp.broadcast_to(sums[e : e + 1, :], (8, z.ec))


def frame_rows(z, place, ne_in, qx_in, qy_in, wx_in, sums_in, edge, a_keep, a_send, b_keep, b_send, cor_a, cor_b, ne, qx, qy, wx, msg, acc, sums):
    core, odd = place[0], place[2]
    lane = lane_iota((8, LANES))
    sub = lax.broadcasted_iota(jnp.int32, (8, z.c), 0)
    per = LANES // (2 * M)
    q4 = z.rest

    for keep, send, first in ((a_keep, a_send, (1 - odd) * (M + z.r)), (b_keep, b_send, odd * (M + z.r))):
        for i in range(M):
            e = NE0 + first + i
            for bt in range(z.ft):
                ne[e, core * z.ft + bt, :, 0 : z.c] = keep[z.ft * i + bt]
                ne[e, (1 - core) * z.ft + bt, :, 0 : z.c] = send[z.ft * i + bt]
            k, s = keep[z.ft * M + i // 2], send[z.ft * M + i // 2]
            k0, s0 = jnp.where(core == 0, k, s), jnp.where(core == 0, s, k)
            if i % 2 == 0:
                s0 = pltpu.roll(s0, q4, axis=0)
            else:
                k0 = pltpu.roll(k0, q4, axis=0)
            ne[e, 2 * z.ft, :, 0 : z.c] = jnp.where(sub < q4, k0, s0)

    n_cor = cor_a.shape[0] - z.lt
    below = [jnp.where(odd == 0, cor_a[v], cor_b[v]) for v in range(n_cor + z.lt)]
    above = [jnp.where(odd == 0, cor_b[v], cor_a[v]) for v in range(n_cor + z.lt)]

    def corner(got, k):
        v, p = divmod(k, per)
        moved = pltpu.roll(got[v], (LANES - M - p * 2 * M) % LANES, axis=1)
        return jnp.where((lane < M) | (lane >= LANES - M), moved, 0.0)

    for r in range(M):
        for t in range(z.bt):
            ne[NE0 + M + z.r + r, t, :, z.c : z.ec] = corner(below, r * z.bt + t)
            ne[NE0 + r, t, :, z.c : z.ec] = corner(above, r * z.bt + t)
    wx[...] = wx_in[...]
    for t in range(z.lt):
        lanes = slice(t * LANES, (t + 1) * LANES)
        wx[M + z.r : z.er, lanes] = below[n_cor + t][0:M]
        wx[0:M, lanes] = above[n_cor + t][8 - M : 8]
    wx[M + z.r : z.er, z.c : z.ec] = corner(below, M * z.bt)[0:M]
    wx[0:M, z.c : z.ec] = corner(above, M * z.bt)[8 - M : 8]
    sums[...] = sums_in[...]
    first_q(z, ne, edge, [(0, M), (M + z.r - 1, z.er - 1)], qx, qy, acc, sums)
    pack_message(z, 0, sums, msg)


CARRY = 1.0 / (1.0 + TAU)
GAIN = TAU / (1.0 + TAU)


def rest_of_update(z, k, ne, u, base):
    def band_tile(t, _):
        for e in range(k + 1, z.er - 1 - k):
            base[NE0 + e, t] = CARRY * u[U0 + e, t] + GAIN * ne[NE0 + e, t]
        return 0

    lax.fori_loop(0, z.bt, band_tile, 0)


def step(z, k, base, wx, edge, u_in, qx_in, qy_in, msg_a, msg_b, u, qx, qy, msg, sums, scale, acc, ubs, pxs, pys):
    lo, hi = k, z.er - 1 - k
    read_scale(z, k, msg_a, msg_b, wx, sums, scale)
    acc[...] = jnp.zeros_like(acc)
    across, along = masks(z, edge)

    def band_tile(t, _):
        px0 = scale[lo] * qx_in[QX0 + lo, t]
        for e in range(lo + 1, hi):
            sc = scale[e]
            px = sc * qx_in[QX0 + e, t]
            py = sc * qy_in[QY0 + e, t]
            div = ((px - px0) + py) - pltpu.roll(py, 1, axis=1)
            old = u_in[(NE0 if k == 0 else U0) + e, t]
            new = (old if k == 0 else base[NE0 + e, t]) + (GAIN * SIGMA) * div
            u[U0 + e, t] = new
            ubs[e] = (new - old) + new
            pxs[e], pys[e] = px, py
            px0 = px
        ub0 = ubs[lo + 1]
        for e in range(lo + 1, hi - 1):
            ub = ubs[e + 1]
            nx = pxs[e] + across(e, ub - ub0)
            ny = pys[e] + along(pltpu.roll(ub0, z.ec - 1, axis=1) - ub0)
            qx[QX0 + e, t] = nx
            qy[QY0 + e, t] = ny
            acc[e] = acc[e] + (nx * nx + ny * ny)
            ub0 = ub
        return 0

    lax.fori_loop(0, z.bt, band_tile, 0)
    write_message(z, k + 1, acc, sums, msg)


def last_step(z, k, own, place, base, wx, qx_in, qy_in, msg_a, msg_b, *refs):
    part = refs[0]
    sums, scale, u = refs[-3:]
    lo, hi = k, z.er - 1 - k
    core = place[0]
    slot = (core if own else 1 - core) * z.ft
    q4 = z.rest
    read_scale(z, k, msg_a, msg_b, wx, sums, scale)

    def band_tile(i, _):
        t = jnp.where(i == z.ft, 2 * z.ft, slot + i)
        px0 = scale[lo] * qx_in[QX0 + lo, t]
        for e in range(lo + 1, hi):
            sc = scale[e]
            px = sc * qx_in[QX0 + e, t]
            py = sc * qy_in[QY0 + e, t]
            div = ((px - px0) + py) - pltpu.roll(py, 1, axis=1)
            new = base[NE0 + e, t] + (GAIN * SIGMA) * div
            u[e - M, i] = new[:, 0 : z.c]
            px0 = px
        return 0

    lax.fori_loop(0, z.ft + 1, band_tile, 0)
    low = (core == 0) if own else (core == 1)
    for r in range(z.r):
        g, q = divmod(r, 8)
        for t in range(z.lt):
            lanes = slice(t * LANES, (t + 1) * LANES)
            run = flat_rows(part, g, t)
            for bt in range(z.ft):
                run[pl.ds(64 * bt + q, 8, stride=8), :] = u[r, bt, :, lanes]
            a, b = u[r, z.ft, 0:q4, lanes], u[r, z.ft, q4:8, lanes]
            run[pl.ds(8 * z.full + q, q4, stride=8), :] = jnp.where(low, a, b)


def write_half(z, own, place, block, *refs):
    out, sem = refs[-2:]
    copies = half_copies(z, place[1] if own else 1 - place[1], out, block, sem, out=True)
    for c in copies:
        c.start()
    for c in copies:
        c.wait()


def local(noisy, weight_map):
    z = Sizes(*noisy.shape)
    n_row, n_col, n_band = (lax.axis_size(a) for a in ("row", "col", "band"))
    chips = n_band // 2
    _, half, _ = here()
    row0 = lax.axis_index("row") * z.r
    col0 = lax.axis_index("col") * (2 * z.c) + half * z.c

    lane = jnp.arange(z.ec)
    gcol = col0 + jnp.where(lane < z.c + LANES // 2, lane, lane - z.ec)
    inner = (gcol >= 0) & (gcol < n_col * 2 * z.c - 1)
    edge = jnp.stack([
        jnp.broadcast_to(row0 > 0, (z.ec,)), jnp.broadcast_to(row0 + z.r < n_row * z.r, (z.ec,)), inner,
    ] + [inner] * 5).astype(F32)

    def at(chip, h):
        return 2 * chip + (h ^ (chip % 2))

    swap = [(i, i ^ 1) for i in range(n_band)]
    pair_a = [(at(c, h), at(c ^ 1, h)) for c in range(chips) for h in range(2)]
    pair_b = [(at(c, h), at((c - 1 + 2 * (c % 2)) % chips, h)) for c in range(chips) for h in range(2)]
    rows_a = [(i, i ^ 1) for i in range(n_row)]
    rows_b = [(i, min(max(i - 1 + 2 * (i % 2), 0), n_row - 1)) for i in range(n_row)]
    across_a = [(i * n_band + b, j * n_band + (b ^ 1)) for i, j in rows_a for b in range(n_band)]
    across_b = [(i * n_band + b, j * n_band + (b ^ 1)) for i, j in rows_b for b in range(n_band)]
    spot = [[(j // 2) * n_band + at(c, j % 2) for j in range(2 * n_col)] for c in range(chips)]
    to_right = [(line[j], line[(j + 1) % len(line)]) for line in spot for j in range(len(line))]
    to_left = [(b, a) for a, b in to_right]

    (edge,) = lax.optimization_barrier((edge,))

    units = z.r * z.bt + z.r // 8
    n_edge = -(-units // (LANES // M))
    n_corner = -(-(M * z.bt + 1) // (LANES // (2 * M)))
    state = (z.er + 4, z.bt, 8, z.ec)
    flat = (z.er, z.ec)
    side = (n_edge, 8, LANES)
    bulk = (z.ft * M + M * z.rest // 8, 8, z.c)
    corner = (n_corner + z.lt, 8, LANES)
    cost = z.er * z.nb * z.ec
    sem = pltpu.SemaphoreType.DMA((z.rg * z.lt,))

    block = (z.lt, z.b, 8, LANES)
    sem_g = pltpu.SemaphoreType.DMA((z.lt,))
    cube, weights = (pltpu.with_memory_space_constraint(x, pltpu.HBM) for x in (noisy, weight_map))
    parts, far = [], []
    for name, same, cross in (("a", rows_a, across_a), ("b", rows_b, across_b)):
        b = name == "b"
        keep, send, msg_keep, msg_send, *w = call(
            lambda *a, b=b: split(z, b, here(), *a), [block, block, bulk, bulk] + [(z.r, z.c)] * b,
            [cube, edge] + [weights] * b, scratch=[sem_g, sem_g] + [pltpu.SemaphoreType.DMA] * b,
            hbm_in=(0, 2), flops=cost,
        )
        far.append(lax.ppermute(msg_keep, "row", same))
        far.append(lax.ppermute(msg_send, ("row", "band"), cross))
        parts += [keep, lax.ppermute(send, "band", swap)]
    (w,) = w
    ne, col_l, col_r = call(
        lambda *a: assemble(z, here(), *a), [state, side, side], [*parts, w, edge], flops=cost
    )
    from_r = lax.ppermute(col_l, ("col", "band"), to_left)
    from_l = lax.ppermute(col_r, ("col", "band"), to_right)
    acc = pltpu.VMEM((z.er, 8, z.ec), F32)
    one = pltpu.VMEM(flat, F32)
    ne, wx, qx, qy, sums, cor_a, cor_b = call(
        lambda *a: frame_cols(z, here(), *a), [state, flat, state, state, flat, corner, corner],
        [ne, w, edge, from_r, from_l], aliases={0: 0}, scratch=[acc], flops=5 * cost,
    )
    cor_a = lax.ppermute(cor_a, "row", rows_a)
    cor_b = lax.ppermute(cor_b, "row", rows_b)
    ne, qx, qy, wx, msg = call(
        lambda *a: frame_rows(z, here(), *a), [state, state, state, flat, message_shape(z, 0)],
        [ne, qx, qy, wx, sums, edge, *far, cor_a, cor_b],
        aliases={0: 0, 1: 1, 2: 2}, scratch=[acc, one], flops=5 * cost,
    )
    u = base = ne
    for k in range(ITERS):
        msg = msg + lax.ppermute(msg, "band", pair_a)
        other = lax.ppermute(msg, "band", pair_b)
        if k > 0:
            (base,) = call(lambda *a, k=k: rest_of_update(z, k, *a), [state], [ne, u], flops=cost)
        if k < ITERS - 1:
            u, qx, qy, msg = call(
                lambda *a, k=k: step(z, k, *a), [state, state, state, message_shape(z, k + 1)],
                [base, wx, edge, u, qx, qy, msg, other], scratch=[one, acc, acc, acc, acc, acc], flops=20 * cost,
            )
    last = [base, wx, qx, qy, msg, other]
    room = [one, acc, pltpu.VMEM((z.r, z.ft + 1, 8, z.c), F32)]
    (send,) = call(lambda *a: last_step(z, ITERS - 1, False, here(), *a), [z.block], last, scratch=room, flops=5 * cost)
    recv = lax.ppermute(send, "band", swap)
    (keep,) = call(lambda *a: last_step(z, ITERS - 1, True, here(), *a), [z.block], last, scratch=room, flops=5 * cost)
    (out,) = call(
        lambda *a: write_half(z, True, here(), *a), [noisy.shape], [keep], scratch=[sem], hbm_out=(0,), flops=cost
    )
    (out,) = call(
        lambda *a: write_half(z, False, here(), *a), [noisy.shape], [recv, out],
        aliases={1: 0}, scratch=[sem], hbm_in=(1,), hbm_out=(0,), flops=cost,
    )
    return out


def solution(mesh):
    placed = (P("band", "row", "col"), P("row", "col"))
    return jax.shard_map(local, mesh=mesh, in_specs=placed, out_specs=P("band", "row", "col"), check_vma=False)
```

profile of v0, /device:TPU:63, one launch (start us, length us, event | category | flops | bytes accessed | tf_op | source)
XLA Modules:
  0.0 87.1 jit_solution(12066518593575097547)
XLA Ops:
  0.1 1.4 %shard_map.28 = (f32[4,28,8,128]{3,2,1,0:T(8,128)S(1)}, f32[4,28,8,128]{3,2,1,0:T(8,128)S(1)}, f32[14,8,512]{2,1,0:T(8,128)S(1)}, f32[14,8,512]{2,1,0:T(8,128)S(1)}) custom-call(f32[28,16,1024]{2,1,0:T(8,128)} %a_0_.3, f32[8,640]{1,0:T(8,128)S(1)} %convert_element_type.3.a_1_.a_5_.a_2_), custom_call_target="tpu_custom_call" | custom-call | flops 860160 | tf_op jit(solution)/shard_map/pallas_call | solution.py:26
  2.3 1.4 %shard_map.29 = (f32[4,28,8,128]{3,2,1,0:T(8,128)S(1)}, f32[4,28,8,128]{3,2,1,0:T(8,128)S(1)}, f32[14,8,512]{2,1,0:T(8,128)S(1)}, f32[14,8,512]{2,1,0:T(8,128)S(1)}, f32[16,512]{1,0:T(8,128)S(1)}) custom-call(f32[28,16,1024]{2,1,0:T(8,128)} %a_0_.3, f32[8,640]{1,0:T(8,128)S(1)} %convert_element_type.3.a_1_.a_5_.a_2_, f32[16,1024]{1,0:T(8,128)} %a_2_.1), custom_call_target="tpu_custom_call" | custom-call | flops 860160 | tf_op jit(solution)/shard_map/pallas_call | solution.py:26
  4.0 2.0 %collective-permute-start.5 = (f32[14,8,512]{2,1,0:T(8,128)S(1)}, f32[14,8,512]{2,1,0:T(8,128)S(1)}, u32[]{:S(2)}, u32[]{:S(2)}) collective-permute-start(f32[14,8,512]{2,1,0:T(8,128)S(1)} %get-tuple-element.55), channel_id=1, source_target_pairs={{0,33},{1,32},{2,35},{3,34},{4,37},{5,36},{6,39},{7,38},{32,1},{33... | collective-permute-start | bytes 688136 | tf_op jit(solution)/shard_map/ppermute | solution.py:460
  8.1 3.9 %collective-permute-done.2.a_3_ = f32[4,8,128]{2,1,0:T(8,128)S(1)} collective-permute-done((f32[4,8,128]{2,1,0:T(8,128)S(1)}, f32[4,8,128]{2,1,0:T(8,128)S(1)}, u32[]{:S(2)}, u32[]{:S(2)}) %collective-permute-start.2) | collective-permute-done | bytes 16416 | tf_op jit(solution)/shard_map/ppermute | solution.py:466
  12.0 1.2 %collective-permute-done.3.a_4_ = f32[4,8,128]{2,1,0:T(8,128)S(1)} collective-permute-done((f32[4,8,128]{2,1,0:T(8,128)S(1)}, f32[4,8,128]{2,1,0:T(8,128)S(1)}, u32[]{:S(2)}, u32[]{:S(2)}) %collective-permute-start.3) | collective-permute-done | bytes 16416 | tf_op jit(solution)/shard_map/ppermute | solution.py:467
  13.1 1.6 %shard_map.31 = (f32[28,7,8,640]{3,2,1,0:T(8,128)S(1)}, f32[24,640]{1,0:T(8,128)S(1)}, f32[28,7,8,640]{3,2,1,0:T(8,128)S(1)}, f32[28,7,8,640]{3,2,1,0:T(8,128)S(...) custom-call(f32[28,7,8,640]{3,2,1,0:T(8,128)S(1)} %get-tuple-element, ...), custom_call_target="tpu_custom_call", output_to_operand_aliasing={{0}: (0, {})} | custom-call | flops 4300800 | tf_op jit(solution)/shard_map/pallas_call | solution.py:26
  14.7 3.9 %collective-permute-start.8 = (f32[6,8,128]{2,1,0:T(8,128)S(1)}, f32[6,8,128]{2,1,0:T(8,128)S(1)}, u32[]{:S(2)}, u32[]{:S(2)}) collective-permute-start(f32[6,8,128]{2,1,0:T(8,128)S(1)} %get-tuple-element.58), channel_id=1, source_target_pairs={{0,32},{32,0},{64,96},{96,64},{128,160},{160,128},{192,224},{224,1... | collective-permute-start | bytes 73736 | tf_op jit(solution)/shard_map/ppermute | solution.py:474
  19.4 6.3 %collective-permute-done.8.a_10_ = f32[6,8,128]{2,1,0:T(8,128)S(1)} collective-permute-done((f32[6,8,128]{2,1,0:T(8,128)S(1)}, f32[6,8,128]{2,1,0:T(8,128)S(1)}, u32[]{:S(2)}, u32[]{:S(2)}) %collective-permute-start.8) | collective-permute-done | bytes 24608 | tf_op jit(solution)/shard_map/ppermute | solution.py:474
  26.8 4.7 %collective-permute-start.10 = (f32[104,128]{1,0:T(8,128)S(1)}, f32[104,128]{1,0:T(8,128)S(1)}, u32[]{:S(2)}, u32[]{:S(2)}) collective-permute-start(f32[104,128]{1,0:T(8,128)S(1)} %get-tuple-element.64), channel_id=1, source_target_pairs={{0,3},{1,2},{3,0},{2,1},{4,7},{5,6},{7,4},{6,5},{8,11},{9,10},{11,... | collective-permute-start | bytes 159752 | tf_op jit(solution)/shard_map/ppermute | solution.py:483
  31.5 1.9 %collective-permute-done.10 = f32[104,128]{1,0:T(8,128)S(1)} collective-permute-done((f32[104,128]{1,0:T(8,128)S(1)}, f32[104,128]{1,0:T(8,128)S(1)}, u32[]{:S(2)}, u32[]{:S(2)}) %collective-permute-start.10) | collective-permute-done | bytes 53280 | tf_op jit(solution)/shard_map/ppermute | solution.py:483
  33.4 6.0 %collective-permute-start.11 = (f32[104,128]{1,0:T(8,128)S(1)}, f32[104,128]{1,0:T(8,128)S(1)}, u32[]{:S(2)}, u32[]{:S(2)}) collective-permute-start(f32[104,128]{1,0:T(8,128)S(1)} %add.43.a_6_), channel_id=1, source_target_pairs={{0,7},{1,6},{3,4},{2,5},{4,3},{5,2},{7,0},{6,1},{8,15},{9,14},{11,... | collective-permute-start | bytes 159752 | tf_op jit(solution)/shard_map/ppermute | solution.py:484
  39.4 2.3 %collective-permute-done.11.a_7_ = f32[104,128]{1,0:T(8,128)S(1)} collective-permute-done((f32[104,128]{1,0:T(8,128)S(1)}, f32[104,128]{1,0:T(8,128)S(1)}, u32[]{:S(2)}, u32[]{:S(2)}) %collective-permute-start.11) | collective-permute-done | bytes 53280 | tf_op jit(solution)/shard_map/ppermute | solution.py:484
  41.7 3.1 %shard_map.33 = (f32[28,7,8,640]{3,2,1,0:T(8,128)S(1)}, f32[28,7,8,640]{3,2,1,0:T(8,128)S(1)}, f32[28,7,8,640]{3,2,1,0:T(8,128)S(1)}, f32[96,128]{1,0:T(8,128)S(1)}) custom-call(f32[28,7,8,640]{3,2,1,0:T(8,128)S(1)} %get-tuple-element.60.a_0_.a_3_, f32[24,640]{1,0:T(8,128)S(1)} %get-tuple-element.61.a_1_, f32[8,640]{1,0:T(8,128)S(1)} %convert_element_type.3.a_1_.a_5_.a_2_, ...), custom_call_target="tpu_custom_call" | custom-call | flops 17203200 | tf_op jit(solution)/shard_map/pallas_call | solution.py:26
  45.6 3.5 %collective-permute-done.12 = f32[96,128]{1,0:T(8,128)S(1)} collective-permute-done((f32[96,128]{1,0:T(8,128)S(1)}, f32[96,128]{1,0:T(8,128)S(1)}, u32[]{:S(2)}, u32[]{:S(2)}) %collective-permute-start.12) | collective-permute-done | bytes 49184 | tf_op jit(solution)/shard_map/ppermute | solution.py:483
  49.2 4.5 %collective-permute-start.13 = (f32[96,128]{1,0:T(8,128)S(1)}, f32[96,128]{1,0:T(8,128)S(1)}, u32[]{:S(2)}, u32[]{:S(2)}) collective-permute-start(f32[96,128]{1,0:T(8,128)S(1)} %add.44.a_6_), channel_id=1, source_target_pairs={{0,7},{1,6},{3,4},{2,5},{4,3},{5,2},{7,0},{6,1},{8,15},{9,14},{11,... | collective-permute-start | bytes 147464 | tf_op jit(solution)/shard_map/ppermute | solution.py:484
  54.2 1.4 %collective-permute-done.13.a_7_ = f32[96,128]{1,0:T(8,128)S(1)} collective-permute-done((f32[96,128]{1,0:T(8,128)S(1)}, f32[96,128]{1,0:T(8,128)S(1)}, u32[]{:S(2)}, u32[]{:S(2)}) %collective-permute-start.13) | collective-permute-done | bytes 49184 | tf_op jit(solution)/shard_map/ppermute | solution.py:484
  55.6 2.9 %shard_map.35 = (f32[28,7,8,640]{3,2,1,0:T(8,128)S(1)}, f32[28,7,8,640]{3,2,1,0:T(8,128)S(1)}, f32[28,7,8,640]{3,2,1,0:T(8,128)S(1)}, f32[88,128]{1,0:T(8,128)S(1)}) custom-call(f32[28,7,8,640]{3,2,1,0:T(8,128)S(1)} %shard_map.34.a_0_, f32[24,640]{1,0:T(8,128)S(1)} %get-tuple-element.61.a_1_, f32[8,640]{1,0:T(8,128)S(1)} %convert_element_type.3.a_1_.a_5_.a_2_, ...), custom_call_target="tpu_custom_call" | custom-call | flops 17203200 | tf_op jit(solution)/shard_map/pallas_call | solution.py:26
  58.7 4.1 %collective-permute-done.14 = f32[88,128]{1,0:T(8,128)S(1)} collective-permute-done((f32[88,128]{1,0:T(8,128)S(1)}, f32[88,128]{1,0:T(8,128)S(1)}, u32[]{:S(2)}, u32[]{:S(2)}) %collective-permute-start.14) | collective-permute-done | bytes 45088 | tf_op jit(solution)/shard_map/ppermute | solution.py:483
  62.9 4.9 %collective-permute-start.15 = (f32[88,128]{1,0:T(8,128)S(1)}, f32[88,128]{1,0:T(8,128)S(1)}, u32[]{:S(2)}, u32[]{:S(2)}) collective-permute-start(f32[88,128]{1,0:T(8,128)S(1)} %add.45.a_6_), channel_id=1, source_target_pairs={{0,7},{1,6},{3,4},{2,5},{4,3},{5,2},{7,0},{6,1},{8,15},{9,14},{11,... | collective-permute-start | bytes 135176 | tf_op jit(solution)/shard_map/ppermute | solution.py:484
  68.2 1.3 %collective-permute-done.15.a_7_ = f32[88,128]{1,0:T(8,128)S(1)} collective-permute-done((f32[88,128]{1,0:T(8,128)S(1)}, f32[88,128]{1,0:T(8,128)S(1)}, u32[]{:S(2)}, u32[]{:S(2)}) %collective-permute-start.15) | collective-permute-done | bytes 45088 | tf_op jit(solution)/shard_map/ppermute | solution.py:484
  69.5 2.7 %shard_map.37 = (f32[28,7,8,640]{3,2,1,0:T(8,128)S(1)}, f32[28,7,8,640]{3,2,1,0:T(8,128)S(1)}, f32[28,7,8,640]{3,2,1,0:T(8,128)S(1)}, f32[80,128]{1,0:T(8,128)S(1)}) custom-call(f32[28,7,8,640]{3,2,1,0:T(8,128)S(1)} %shard_map.36.a_0_, f32[24,640]{1,0:T(8,128)S(1)} %get-tuple-element.61.a_1_, f32[8,640]{1,0:T(8,128)S(1)} %convert_element_type.3.a_1_.a_5_.a_2_, ...), custom_call_target="tpu_custom_call" | custom-call | flops 17203200 | tf_op jit(solution)/shard_map/pallas_call | solution.py:26
  72.3 4.2 %collective-permute-done.16 = f32[80,128]{1,0:T(8,128)S(1)} collective-permute-done((f32[80,128]{1,0:T(8,128)S(1)}, f32[80,128]{1,0:T(8,128)S(1)}, u32[]{:S(2)}, u32[]{:S(2)}) %collective-permute-start.16) | collective-permute-done | bytes 40992 | tf_op jit(solution)/shard_map/ppermute | solution.py:483
  76.5 4.2 %collective-permute-start.17 = (f32[80,128]{1,0:T(8,128)S(1)}, f32[80,128]{1,0:T(8,128)S(1)}, u32[]{:S(2)}, u32[]{:S(2)}) collective-permute-start(f32[80,128]{1,0:T(8,128)S(1)} %add.46.a_4_), channel_id=1, source_target_pairs={{0,7},{1,6},{3,4},{2,5},{4,3},{5,2},{7,0},{6,1},{8,15},{9,14},{11,... | collective-permute-start | bytes 122888 | tf_op jit(solution)/shard_map/ppermute | solution.py:484
  81.1 1.3 %collective-permute-done.17.a_5_ = f32[80,128]{1,0:T(8,128)S(1)} collective-permute-done((f32[80,128]{1,0:T(8,128)S(1)}, f32[80,128]{1,0:T(8,128)S(1)}, u32[]{:S(2)}, u32[]{:S(2)}) %collective-permute-start.17) | collective-permute-done | bytes 40992 | tf_op jit(solution)/shard_map/ppermute | solution.py:484
  (38 shorter events, 12.1 us)
Async XLA Ops:
  1.6 5.1 %collective-permute-start = (f32[4,28,8,128]{3,2,1,0:T(8,128)S(1)}, f32[4,28,8,128]{3,2,1,0:T(8,128)S(1)}, u32[]{:S(2)}, u32[]{:S(2)}) collective-permute-start(f32[4,28,8,128]{3,2,1,0:T(8,128)S(1)} %get-tuple-element.42), channel_id=1, source_target_pairs={{0,1},{1,0},{2,3},{3,2},{4,5},{5,4},{6,7},{7,6},{8,9},{9,8},{10,11... | collective-permute-start | bytes 1376264 | tf_op jit(solution)/shard_map/ppermute | solution.py:461
  3.8 3.0 %collective-permute-start.1 = (f32[4,28,8,128]{3,2,1,0:T(8,128)S(1)}, f32[4,28,8,128]{3,2,1,0:T(8,128)S(1)}, u32[]{:S(2)}, u32[]{:S(2)}) collective-permute-start(f32[4,28,8,128]{3,2,1,0:T(8,128)S(1)} %get-tuple-element.44), channel_id=1, source_target_pairs={{0,1},{1,0},{2,3},{3,2},{4,5},{5,4},{6,7},{7,6},{8,9},{9,8},{10,11... | collective-permute-start | bytes 1376264 | tf_op jit(solution)/shard_map/ppermute | solution.py:461
  3.9 14.8 %collective-permute-start.4 = (f32[14,8,512]{2,1,0:T(8,128)S(1)}, f32[14,8,512]{2,1,0:T(8,128)S(1)}, u32[]{:S(2)}, u32[]{:S(2)}) collective-permute-start(f32[14,8,512]{2,1,0:T(8,128)S(1)} %get-tuple-element.54), channel_id=1, source_target_pairs={{0,32},{32,0},{64,96},{96,64},{128,160},{160,128},{192,224},{224,1... | collective-permute-start | bytes 688136 | tf_op jit(solution)/shard_map/ppermute | solution.py:459
  4.0 15.4 %collective-permute-start.5 = (f32[14,8,512]{2,1,0:T(8,128)S(1)}, f32[14,8,512]{2,1,0:T(8,128)S(1)}, u32[]{:S(2)}, u32[]{:S(2)}) collective-permute-start(f32[14,8,512]{2,1,0:T(8,128)S(1)} %get-tuple-element.55), channel_id=1, source_target_pairs={{0,33},{1,32},{2,35},{3,34},{4,37},{5,36},{6,39},{7,38},{32,1},{33... | collective-permute-start | bytes 688136 | tf_op jit(solution)/shard_map/ppermute | solution.py:460
  6.0 13.3 %collective-permute-start.6 = (f32[14,8,512]{2,1,0:T(8,128)S(1)}, f32[14,8,512]{2,1,0:T(8,128)S(1)}, u32[]{:S(2)}, u32[]{:S(2)}) collective-permute-start(f32[14,8,512]{2,1,0:T(8,128)S(1)} %get-tuple-element.56), channel_id=1, source_target_pairs={{0,0},{32,64},{64,32},{96,128},{128,96},{160,192},{192,160},{224,2... | collective-permute-start | bytes 688136 | tf_op jit(solution)/shard_map/ppermute | solution.py:459
  6.7 12.7 %collective-permute-start.7 = (f32[14,8,512]{2,1,0:T(8,128)S(1)}, f32[14,8,512]{2,1,0:T(8,128)S(1)}, u32[]{:S(2)}, u32[]{:S(2)}) collective-permute-start(f32[14,8,512]{2,1,0:T(8,128)S(1)} %get-tuple-element.57), channel_id=1, source_target_pairs={{0,1},{1,0},{2,3},{3,2},{4,5},{5,4},{6,7},{7,6},{32,65},{33,64},{3... | collective-permute-start | bytes 688136 | tf_op jit(solution)/shard_map/ppermute | solution.py:460
  7.5 4.5 %collective-permute-start.2 = (f32[4,8,128]{2,1,0:T(8,128)S(1)}, f32[4,8,128]{2,1,0:T(8,128)S(1)}, u32[]{:S(2)}, u32[]{:S(2)}) collective-permute-start(f32[4,8,128]{2,1,0:T(8,128)S(1)} %get-tuple-element.47), channel_id=1, source_target_pairs={{1,0},{8,1},{9,8},{16,9},{17,16},{24,17},{25,24},{0,25},{2,3},{11,... | collective-permute-start | bytes 49160 | tf_op jit(solution)/shard_map/ppermute | solution.py:466
  11.9 1.2 %collective-permute-start.3 = (f32[4,8,128]{2,1,0:T(8,128)S(1)}, f32[4,8,128]{2,1,0:T(8,128)S(1)}, u32[]{:S(2)}, u32[]{:S(2)}) collective-permute-start(f32[4,8,128]{2,1,0:T(8,128)S(1)} %get-tuple-element.48), channel_id=1, source_target_pairs={{0,1},{1,8},{8,9},{9,16},{16,17},{17,24},{24,25},{25,0},{3,2},{2,1... | collective-permute-start | bytes 49160 | tf_op jit(solution)/shard_map/ppermute | solution.py:467
  14.7 11.0 %collective-permute-start.8 = (f32[6,8,128]{2,1,0:T(8,128)S(1)}, f32[6,8,128]{2,1,0:T(8,128)S(1)}, u32[]{:S(2)}, u32[]{:S(2)}) collective-permute-start(f32[6,8,128]{2,1,0:T(8,128)S(1)} %get-tuple-element.58), channel_id=1, source_target_pairs={{0,32},{32,0},{64,96},{96,64},{128,160},{160,128},{192,224},{224,1... | collective-permute-start | bytes 73736 | tf_op jit(solution)/shard_map/ppermute | solution.py:474
  18.7 7.0 %collective-permute-start.9 = (f32[6,8,128]{2,1,0:T(8,128)S(1)}, f32[6,8,128]{2,1,0:T(8,128)S(1)}, u32[]{:S(2)}, u32[]{:S(2)}) collective-permute-start(f32[6,8,128]{2,1,0:T(8,128)S(1)} %get-tuple-element.59), channel_id=1, source_target_pairs={{0,0},{32,64},{64,32},{96,128},{128,96},{160,192},{192,160},{224,2... | collective-permute-start | bytes 73736 | tf_op jit(solution)/shard_map/ppermute | solution.py:475
  26.8 6.6 %collective-permute-start.10 = (f32[104,128]{1,0:T(8,128)S(1)}, f32[104,128]{1,0:T(8,128)S(1)}, u32[]{:S(2)}, u32[]{:S(2)}) collective-permute-start(f32[104,128]{1,0:T(8,128)S(1)} %get-tuple-element.64), channel_id=1, source_target_pairs={{0,3},{1,2},{3,0},{2,1},{4,7},{5,6},{7,4},{6,5},{8,11},{9,10},{11,... | collective-permute-start | bytes 159752 | tf_op jit(solution)/shard_map/ppermute | solution.py:483
  33.4 8.2 %collective-permute-start.11 = (f32[104,128]{1,0:T(8,128)S(1)}, f32[104,128]{1,0:T(8,128)S(1)}, u32[]{:S(2)}, u32[]{:S(2)}) collective-permute-start(f32[104,128]{1,0:T(8,128)S(1)} %add.43.a_6_), channel_id=1, source_target_pairs={{0,7},{1,6},{3,4},{2,5},{4,3},{5,2},{7,0},{6,1},{8,15},{9,14},{11,... | collective-permute-start | bytes 159752 | tf_op jit(solution)/shard_map/ppermute | solution.py:484
  44.7 4.4 %collective-permute-start.12 = (f32[96,128]{1,0:T(8,128)S(1)}, f32[96,128]{1,0:T(8,128)S(1)}, u32[]{:S(2)}, u32[]{:S(2)}) collective-permute-start(f32[96,128]{1,0:T(8,128)S(1)} %get-tuple-element.68), channel_id=1, source_target_pairs={{0,3},{1,2},{3,0},{2,1},{4,7},{5,6},{7,4},{6,5},{8,11},{9,10},{11,... | collective-permute-start | bytes 147464 | tf_op jit(solution)/shard_map/ppermute | solution.py:483
  49.2 6.4 %collective-permute-start.13 = (f32[96,128]{1,0:T(8,128)S(1)}, f32[96,128]{1,0:T(8,128)S(1)}, u32[]{:S(2)}, u32[]{:S(2)}) collective-permute-start(f32[96,128]{1,0:T(8,128)S(1)} %add.44.a_6_), channel_id=1, source_target_pairs={{0,7},{1,6},{3,4},{2,5},{4,3},{5,2},{7,0},{6,1},{8,15},{9,14},{11,... | collective-permute-start | bytes 147464 | tf_op jit(solution)/shard_map/ppermute | solution.py:484
  58.5 4.4 %collective-permute-start.14 = (f32[88,128]{1,0:T(8,128)S(1)}, f32[88,128]{1,0:T(8,128)S(1)}, u32[]{:S(2)}, u32[]{:S(2)}) collective-permute-start(f32[88,128]{1,0:T(8,128)S(1)} %get-tuple-element.72), channel_id=1, source_target_pairs={{0,3},{1,2},{3,0},{2,1},{4,7},{5,6},{7,4},{6,5},{8,11},{9,10},{11,... | collective-permute-start | bytes 135176 | tf_op jit(solution)/shard_map/ppermute | solution.py:483
  62.9 6.6 %collective-permute-start.15 = (f32[88,128]{1,0:T(8,128)S(1)}, f32[88,128]{1,0:T(8,128)S(1)}, u32[]{:S(2)}, u32[]{:S(2)}) collective-permute-start(f32[88,128]{1,0:T(8,128)S(1)} %add.45.a_6_), channel_id=1, source_target_pairs={{0,7},{1,6},{3,4},{2,5},{4,3},{5,2},{7,0},{6,1},{8,15},{9,14},{11,... | collective-permute-start | bytes 135176 | tf_op jit(solution)/shard_map/ppermute | solution.py:484
  72.2 4.4 %collective-permute-start.16 = (f32[80,128]{1,0:T(8,128)S(1)}, f32[80,128]{1,0:T(8,128)S(1)}, u32[]{:S(2)}, u32[]{:S(2)}) collective-permute-start(f32[80,128]{1,0:T(8,128)S(1)} %get-tuple-element.76), channel_id=1, source_target_pairs={{0,3},{1,2},{3,0},{2,1},{4,7},{5,6},{7,4},{6,5},{8,11},{9,10},{11,... | collective-permute-start | bytes 122888 | tf_op jit(solution)/shard_map/ppermute | solution.py:483
  76.5 5.8 %collective-permute-start.17 = (f32[80,128]{1,0:T(8,128)S(1)}, f32[80,128]{1,0:T(8,128)S(1)}, u32[]{:S(2)}, u32[]{:S(2)}) collective-permute-start(f32[80,128]{1,0:T(8,128)S(1)} %add.46.a_4_), channel_id=1, source_target_pairs={{0,7},{1,6},{3,4},{2,5},{4,3},{5,2},{7,0},{6,1},{8,15},{9,14},{11,... | collective-permute-start | bytes 122888 | tf_op jit(solution)/shard_map/ppermute | solution.py:484
  83.4 2.6 %collective-permute-start.18 = (f32[2,4,28,8,128]{4,3,2,1,0:T(8,128)S(1)}, f32[2,4,28,8,128]{4,3,2,1,0:T(8,128)S(1)}, u32[]{:S(2)}, u32[]{:S(2)}) collective-permute-start(f32[2,4,28,8,128]{4,3,2,1,0:T(8,128)S(1)} %shard_map.39), channel_id=1, source_target_pairs={{0,1},{1,0},{2,3},{3,2},{4,5},{5,4},{6,7},{7,6},{8,9},{9,8},{10,11... | collective-permute-start | bytes 2752520 | tf_op jit(solution)/shard_map/ppermute | solution.py:495
where the time goes:
time: 88.2 us; the launch traced here: 87.1 us
  starting transfers between devices  34.6 us (39%)
  waiting for transfers between devices  31.8 us (36%)
  Pallas kernels  20.2 us (23%)
    pallas_call x15, Pallas kernels, call(): pl.pallas_call(body, out_shape=[(pltpu.HBM if i in hbm_out else pltpu.VME...  20.2 us
    ppermute x4, starting transfers between devices, local(): other = lax.ppermute(msg, 'band', pair_b)  19.5 us
    ppermute x4, waiting for transfers between devices, local(): msg = msg + lax.ppermute(msg, 'band', pair_a)  13.7 us
    ppermute x1, waiting for transfers between devices, local(): cor_a = lax.ppermute(cor_a, 'row', rows_a)  6.33 us
    ppermute x4, waiting for transfers between devices, local(): other = lax.ppermute(msg, 'band', pair_b)  6.3 us
    ppermute x4, starting transfers between devices, local(): msg = msg + lax.ppermute(msg, 'band', pair_a)  6.08 us
    ppermute x1, starting transfers between devices, local(): cor_a = lax.ppermute(cor_a, 'row', rows_a)  3.95 us
    ppermute x1, waiting for transfers between devices, local(): from_r = lax.ppermute(col_l, ('col', 'band'), to_left)  3.89 us
  transfers between devices with their start and end apart: 19, of which 12 were waited for; matrix products, arithmetic and copies ran while one was open for 0% of the time, Pallas kernels for 8%

commit v1 on v0

--- a/solution.py
+++ b/solution.py
@@ -480,8 +480,9 @@
     )
     u = base = ne
     for k in range(ITERS):
-        msg = msg + lax.ppermute(msg, "band", pair_a)
-        other = lax.ppermute(msg, "band", pair_b)
+        pairs = (pair_a, pair_b) if k % 2 == 0 else (pair_b, pair_a)
+        msg = msg + lax.ppermute(msg, "band", pairs[0])
+        other = lax.ppermute(msg, "band", pairs[1])
         if k > 0:
             (base,) = call(lambda *a, k=k: rest_of_update(z, k, *a), [state], [ne, u], flops=cost)
         if k < ITERS - 1:

time: 88.2 us -> 88.3 us (level)
  starting transfers between devices: 34.6 us -> 30.5 us
  waiting for transfers between devices: 31.8 us -> 35.8 us
    ppermute x8, starting transfers between devices: 25.6 us -> 21.5 us  [the longest x4 11.2 us: local(): msg = msg + lax.ppermute(msg, 'band', pairs[0])]
    ppermute x8, waiting for transfers between devices: 20 us -> 24 us  [the longest x4 12.3 us: local(): other = lax.ppermute(msg, 'band', pairs[1])]
where the time goes in v1:
time: 88.3 us; the launch traced here: 87 us
  waiting for transfers between devices  35.8 us (41%)
  starting transfers between devices  30.5 us (35%)
  Pallas kernels  20.2 us (23%)
    pallas_call x15, Pallas kernels, call(): pl.pallas_call(body, out_shape=[(pltpu.HBM if i in hbm_out else pltpu.VME...  20.2 us
    ppermute x4, waiting for transfers between devices, local(): other = lax.ppermute(msg, 'band', pairs[1])  12.3 us
    ppermute x4, waiting for transfers between devices, local(): msg = msg + lax.ppermute(msg, 'band', pairs[0])  11.7 us
    ppermute x4, starting transfers between devices, local(): msg = msg + lax.ppermute(msg, 'band', pairs[0])  11.2 us
    ppermute x4, starting transfers between devices, local(): other = lax.ppermute(msg, 'band', pairs[1])  10.3 us
    ppermute x1, waiting for transfers between devices, local(): cor_a = lax.ppermute(cor_a, 'row', rows_a)  6.33 us
    ppermute x1, starting transfers between devices, local(): cor_a = lax.ppermute(cor_a, 'row', rows_a)  3.95 us
    ppermute x1, waiting for transfers between devices, local(): from_r = lax.ppermute(col_l, ('col', 'band'), to_left)  3.89 us
  transfers between devices with their start and end apart: 19, of which 12 were waited for; matrix products, arithmetic and copies ran while one was open for 0% of the time, Pallas kernels for 8%

profile of v1, /device:TPU:63, one launch (start us, length us, event | category | flops | bytes accessed | tf_op | source)
XLA Modules:
  0.0 87.0 jit_solution(11256787676968319238)
XLA Ops:
  0.1 1.4 %shard_map.28 = (f32[4,28,8,128]{3,2,1,0:T(8,128)S(1)}, f32[4,28,8,128]{3,2,1,0:T(8,128)S(1)}, f32[14,8,512]{2,1,0:T(8,128)S(1)}, f32[14,8,512]{2,1,0:T(8,128)S(1)}) custom-call(f32[28,16,1024]{2,1,0:T(8,128)} %a_0_.3, f32[8,640]{1,0:T(8,128)S(1)} %convert_element_type.3.a_1_.a_5_.a_2_), custom_call_target="tpu_custom_call" | custom-call | flops 860160 | tf_op jit(solution)/shard_map/pallas_call | solution.py:26
  2.3 1.4 %shard_map.29 = (f32[4,28,8,128]{3,2,1,0:T(8,128)S(1)}, f32[4,28,8,128]{3,2,1,0:T(8,128)S(1)}, f32[14,8,512]{2,1,0:T(8,128)S(1)}, f32[14,8,512]{2,1,0:T(8,128)S(1)}, f32[16,512]{1,0:T(8,128)S(1)}) custom-call(f32[28,16,1024]{2,1,0:T(8,128)} %a_0_.3, f32[8,640]{1,0:T(8,128)S(1)} %convert_element_type.3.a_1_.a_5_.a_2_, f32[16,1024]{1,0:T(8,128)} %a_2_.1), custom_call_target="tpu_custom_call" | custom-call | flops 860160 | tf_op jit(solution)/shard_map/pallas_call | solution.py:26
  4.0 2.0 %collective-permute-start.5 = (f32[14,8,512]{2,1,0:T(8,128)S(1)}, f32[14,8,512]{2,1,0:T(8,128)S(1)}, u32[]{:S(2)}, u32[]{:S(2)}) collective-permute-start(f32[14,8,512]{2,1,0:T(8,128)S(1)} %get-tuple-element.55), channel_id=1, source_target_pairs={{0,33},{1,32},{2,35},{3,34},{4,37},{5,36},{6,39},{7,38},{32,1},{33... | collective-permute-start | bytes 688136 | tf_op jit(solution)/shard_map/ppermute | solution.py:460
  8.1 3.9 %collective-permute-done.2.a_3_ = f32[4,8,128]{2,1,0:T(8,128)S(1)} collective-permute-done((f32[4,8,128]{2,1,0:T(8,128)S(1)}, f32[4,8,128]{2,1,0:T(8,128)S(1)}, u32[]{:S(2)}, u32[]{:S(2)}) %collective-permute-start.2) | collective-permute-done | bytes 16416 | tf_op jit(solution)/shard_map/ppermute | solution.py:466
  12.0 1.2 %collective-permute-done.3.a_4_ = f32[4,8,128]{2,1,0:T(8,128)S(1)} collective-permute-done((f32[4,8,128]{2,1,0:T(8,128)S(1)}, f32[4,8,128]{2,1,0:T(8,128)S(1)}, u32[]{:S(2)}, u32[]{:S(2)}) %collective-permute-start.3) | collective-permute-done | bytes 16416 | tf_op jit(solution)/shard_map/ppermute | solution.py:467
  13.1 1.6 %shard_map.31 = (f32[28,7,8,640]{3,2,1,0:T(8,128)S(1)}, f32[24,640]{1,0:T(8,128)S(1)}, f32[28,7,8,640]{3,2,1,0:T(8,128)S(1)}, f32[28,7,8,640]{3,2,1,0:T(8,128)S(...) custom-call(f32[28,7,8,640]{3,2,1,0:T(8,128)S(1)} %get-tuple-element, ...), custom_call_target="tpu_custom_call", output_to_operand_aliasing={{0}: (0, {})} | custom-call | flops 4300800 | tf_op jit(solution)/shard_map/pallas_call | solution.py:26
  14.7 3.9 %collective-permute-start.8 = (f32[6,8,128]{2,1,0:T(8,128)S(1)}, f32[6,8,128]{2,1,0:T(8,128)S(1)}, u32[]{:S(2)}, u32[]{:S(2)}) collective-permute-start(f32[6,8,128]{2,1,0:T(8,128)S(1)} %get-tuple-element.58), channel_id=1, source_target_pairs={{0,32},{32,0},{64,96},{96,64},{128,160},{160,128},{192,224},{224,1... | collective-permute-start | bytes 73736 | tf_op jit(solution)/shard_map/ppermute | solution.py:474
  19.4 6.3 %collective-permute-done.8.a_10_ = f32[6,8,128]{2,1,0:T(8,128)S(1)} collective-permute-done((f32[6,8,128]{2,1,0:T(8,128)S(1)}, f32[6,8,128]{2,1,0:T(8,128)S(1)}, u32[]{:S(2)}, u32[]{:S(2)}) %collective-permute-start.8) | collective-permute-done | bytes 24608 | tf_op jit(solution)/shard_map/ppermute | solution.py:474
  26.8 4.7 %collective-permute-start.10 = (f32[104,128]{1,0:T(8,128)S(1)}, f32[104,128]{1,0:T(8,128)S(1)}, u32[]{:S(2)}, u32[]{:S(2)}) collective-permute-start(f32[104,128]{1,0:T(8,128)S(1)} %get-tuple-element.64), channel_id=1, source_target_pairs={{0,3},{1,2},{3,0},{2,1},{4,7},{5,6},{7,4},{6,5},{8,11},{9,10},{11,... | collective-permute-start | bytes 159752 | tf_op jit(solution)/shard_map/ppermute | solution.py:484
  31.5 1.9 %collective-permute-done.10 = f32[104,128]{1,0:T(8,128)S(1)} collective-permute-done((f32[104,128]{1,0:T(8,128)S(1)}, f32[104,128]{1,0:T(8,128)S(1)}, u32[]{:S(2)}, u32[]{:S(2)}) %collective-permute-start.10) | collective-permute-done | bytes 53280 | tf_op jit(solution)/shard_map/ppermute | solution.py:484
  33.4 6.0 %collective-permute-start.11 = (f32[104,128]{1,0:T(8,128)S(1)}, f32[104,128]{1,0:T(8,128)S(1)}, u32[]{:S(2)}, u32[]{:S(2)}) collective-permute-start(f32[104,128]{1,0:T(8,128)S(1)} %add.43.a_6_), channel_id=1, source_target_pairs={{0,7},{1,6},{3,4},{2,5},{4,3},{5,2},{7,0},{6,1},{8,15},{9,14},{11,... | collective-permute-start | bytes 159752 | tf_op jit(solution)/shard_map/ppermute | solution.py:485
  39.4 2.3 %collective-permute-done.11.a_7_ = f32[104,128]{1,0:T(8,128)S(1)} collective-permute-done((f32[104,128]{1,0:T(8,128)S(1)}, f32[104,128]{1,0:T(8,128)S(1)}, u32[]{:S(2)}, u32[]{:S(2)}) %collective-permute-start.11) | collective-permute-done | bytes 53280 | tf_op jit(solution)/shard_map/ppermute | solution.py:485
  41.7 3.1 %shard_map.33 = (f32[28,7,8,640]{3,2,1,0:T(8,128)S(1)}, f32[28,7,8,640]{3,2,1,0:T(8,128)S(1)}, f32[28,7,8,640]{3,2,1,0:T(8,128)S(1)}, f32[96,128]{1,0:T(8,128)S(1)}) custom-call(f32[28,7,8,640]{3,2,1,0:T(8,128)S(1)} %get-tuple-element.60.a_0_.a_3_, f32[24,640]{1,0:T(8,128)S(1)} %get-tuple-element.61.a_1_, f32[8,640]{1,0:T(8,128)S(1)} %convert_element_type.3.a_1_.a_5_.a_2_, ...), custom_call_target="tpu_custom_call" | custom-call | flops 17203200 | tf_op jit(solution)/shard_map/pallas_call | solution.py:26
  44.7 3.4 %collective-permute-start.12 = (f32[96,128]{1,0:T(8,128)S(1)}, f32[96,128]{1,0:T(8,128)S(1)}, u32[]{:S(2)}, u32[]{:S(2)}) collective-permute-start(f32[96,128]{1,0:T(8,128)S(1)} %get-tuple-element.68), channel_id=1, source_target_pairs={{0,7},{1,6},{3,4},{2,5},{4,3},{5,2},{7,0},{6,1},{8,15},{9,14},{11,... | collective-permute-start | bytes 147464 | tf_op jit(solution)/shard_map/ppermute | solution.py:484
  48.1 2.4 %collective-permute-done.12 = f32[96,128]{1,0:T(8,128)S(1)} collective-permute-done((f32[96,128]{1,0:T(8,128)S(1)}, f32[96,128]{1,0:T(8,128)S(1)}, u32[]{:S(2)}, u32[]{:S(2)}) %collective-permute-start.12) | collective-permute-done | bytes 49184 | tf_op jit(solution)/shard_map/ppermute | solution.py:484
  51.8 3.2 %collective-permute-done.13.a_7_ = f32[96,128]{1,0:T(8,128)S(1)} collective-permute-done((f32[96,128]{1,0:T(8,128)S(1)}, f32[96,128]{1,0:T(8,128)S(1)}, u32[]{:S(2)}, u32[]{:S(2)}) %collective-permute-start.13) | collective-permute-done | bytes 49184 | tf_op jit(solution)/shard_map/ppermute | solution.py:485
  55.1 2.9 %shard_map.35 = (f32[28,7,8,640]{3,2,1,0:T(8,128)S(1)}, f32[28,7,8,640]{3,2,1,0:T(8,128)S(1)}, f32[28,7,8,640]{3,2,1,0:T(8,128)S(1)}, f32[88,128]{1,0:T(8,128)S(1)}) custom-call(f32[28,7,8,640]{3,2,1,0:T(8,128)S(1)} %shard_map.34.a_0_, f32[24,640]{1,0:T(8,128)S(1)} %get-tuple-element.61.a_1_, f32[8,640]{1,0:T(8,128)S(1)} %convert_element_type.3.a_1_.a_5_.a_2_, ...), custom_call_target="tpu_custom_call" | custom-call | flops 17203200 | tf_op jit(solution)/shard_map/pallas_call | solution.py:26
  58.7 3.7 %collective-permute-done.14 = f32[88,128]{1,0:T(8,128)S(1)} collective-permute-done((f32[88,128]{1,0:T(8,128)S(1)}, f32[88,128]{1,0:T(8,128)S(1)}, u32[]{:S(2)}, u32[]{:S(2)}) %collective-permute-start.14) | collective-permute-done | bytes 45088 | tf_op jit(solution)/shard_map/ppermute | solution.py:484
  62.4 3.5 %collective-permute-start.15 = (f32[88,128]{1,0:T(8,128)S(1)}, f32[88,128]{1,0:T(8,128)S(1)}, u32[]{:S(2)}, u32[]{:S(2)}) collective-permute-start(f32[88,128]{1,0:T(8,128)S(1)} %add.45.a_6_), channel_id=1, source_target_pairs={{0,7},{1,6},{3,4},{2,5},{4,3},{5,2},{7,0},{6,1},{8,15},{9,14},{11,... | collective-permute-start | bytes 135176 | tf_op jit(solution)/shard_map/ppermute | solution.py:485
  66.3 2.8 %collective-permute-done.15.a_7_ = f32[88,128]{1,0:T(8,128)S(1)} collective-permute-done((f32[88,128]{1,0:T(8,128)S(1)}, f32[88,128]{1,0:T(8,128)S(1)}, u32[]{:S(2)}, u32[]{:S(2)}) %collective-permute-start.15) | collective-permute-done | bytes 45088 | tf_op jit(solution)/shard_map/ppermute | solution.py:485
  69.2 2.7 %shard_map.37 = (f32[28,7,8,640]{3,2,1,0:T(8,128)S(1)}, f32[28,7,8,640]{3,2,1,0:T(8,128)S(1)}, f32[28,7,8,640]{3,2,1,0:T(8,128)S(1)}, f32[80,128]{1,0:T(8,128)S(1)}) custom-call(f32[28,7,8,640]{3,2,1,0:T(8,128)S(1)} %shard_map.36.a_0_, f32[24,640]{1,0:T(8,128)S(1)} %get-tuple-element.61.a_1_, f32[8,640]{1,0:T(8,128)S(1)} %convert_element_type.3.a_1_.a_5_.a_2_, ...), custom_call_target="tpu_custom_call" | custom-call | flops 17203200 | tf_op jit(solution)/shard_map/pallas_call | solution.py:26
  71.9 2.3 %collective-permute-start.16 = (f32[80,128]{1,0:T(8,128)S(1)}, f32[80,128]{1,0:T(8,128)S(1)}, u32[]{:S(2)}, u32[]{:S(2)}) collective-permute-start(f32[80,128]{1,0:T(8,128)S(1)} %get-tuple-element.76), channel_id=1, source_target_pairs={{0,7},{1,6},{3,4},{2,5},{4,3},{5,2},{7,0},{6,1},{8,15},{9,14},{11,... | collective-permute-start | bytes 122888 | tf_op jit(solution)/shard_map/ppermute | solution.py:484
  74.2 3.7 %collective-permute-done.16 = f32[80,128]{1,0:T(8,128)S(1)} collective-permute-done((f32[80,128]{1,0:T(8,128)S(1)}, f32[80,128]{1,0:T(8,128)S(1)}, u32[]{:S(2)}, u32[]{:S(2)}) %collective-permute-start.16) | collective-permute-done | bytes 40992 | tf_op jit(solution)/shard_map/ppermute | solution.py:484
  78.3 3.9 %collective-permute-done.17.a_5_ = f32[80,128]{1,0:T(8,128)S(1)} collective-permute-done((f32[80,128]{1,0:T(8,128)S(1)}, f32[80,128]{1,0:T(8,128)S(1)}, u32[]{:S(2)}, u32[]{:S(2)}) %collective-permute-start.17) | collective-permute-done | bytes 40992 | tf_op jit(solution)/shard_map/ppermute | solution.py:485
  (38 shorter events, 12.2 us)
Async XLA Ops:
  1.6 5.1 %collective-permute-start = (f32[4,28,8,128]{3,2,1,0:T(8,128)S(1)}, f32[4,28,8,128]{3,2,1,0:T(8,128)S(1)}, u32[]{:S(2)}, u32[]{:S(2)}) collective-permute-start(f32[4,28,8,128]{3,2,1,0:T(8,128)S(1)} %get-tuple-element.42), channel_id=1, source_target_pairs={{0,1},{1,0},{2,3},{3,2},{4,5},{5,4},{6,7},{7,6},{8,9},{9,8},{10,11... | collective-permute-start | bytes 1376264 | tf_op jit(solution)/shard_map/ppermute | solution.py:461
  3.8 3.0 %collective-permute-start.1 = (f32[4,28,8,128]{3,2,1,0:T(8,128)S(1)}, f32[4,28,8,128]{3,2,1,0:T(8,128)S(1)}, u32[]{:S(2)}, u32[]{:S(2)}) collective-permute-start(f32[4,28,8,128]{3,2,1,0:T(8,128)S(1)} %get-tuple-element.44), channel_id=1, source_target_pairs={{0,1},{1,0},{2,3},{3,2},{4,5},{5,4},{6,7},{7,6},{8,9},{9,8},{10,11... | collective-permute-start | bytes 1376264 | tf_op jit(solution)/shard_map/ppermute | solution.py:461
  3.9 14.8 %collective-permute-start.4 = (f32[14,8,512]{2,1,0:T(8,128)S(1)}, f32[14,8,512]{2,1,0:T(8,128)S(1)}, u32[]{:S(2)}, u32[]{:S(2)}) collective-permute-start(f32[14,8,512]{2,1,0:T(8,128)S(1)} %get-tuple-element.54), channel_id=1, source_target_pairs={{0,32},{32,0},{64,96},{96,64},{128,160},{160,128},{192,224},{224,1... | collective-permute-start | bytes 688136 | tf_op jit(solution)/shard_map/ppermute | solution.py:459
  4.0 15.4 %collective-permute-start.5 = (f32[14,8,512]{2,1,0:T(8,128)S(1)}, f32[14,8,512]{2,1,0:T(8,128)S(1)}, u32[]{:S(2)}, u32[]{:S(2)}) collective-permute-start(f32[14,8,512]{2,1,0:T(8,128)S(1)} %get-tuple-element.55), channel_id=1, source_target_pairs={{0,33},{1,32},{2,35},{3,34},{4,37},{5,36},{6,39},{7,38},{32,1},{33... | collective-permute-start | bytes 688136 | tf_op jit(solution)/shard_map/ppermute | solution.py:460
  6.0 13.3 %collective-permute-start.6 = (f32[14,8,512]{2,1,0:T(8,128)S(1)}, f32[14,8,512]{2,1,0:T(8,128)S(1)}, u32[]{:S(2)}, u32[]{:S(2)}) collective-permute-start(f32[14,8,512]{2,1,0:T(8,128)S(1)} %get-tuple-element.56), channel_id=1, source_target_pairs={{0,0},{32,64},{64,32},{96,128},{128,96},{160,192},{192,160},{224,2... | collective-permute-start | bytes 688136 | tf_op jit(solution)/shard_map/ppermute | solution.py:459
  6.7 12.7 %collective-permute-start.7 = (f32[14,8,512]{2,1,0:T(8,128)S(1)}, f32[14,8,512]{2,1,0:T(8,128)S(1)}, u32[]{:S(2)}, u32[]{:S(2)}) collective-permute-start(f32[14,8,512]{2,1,0:T(8,128)S(1)} %get-tuple-element.57), channel_id=1, source_target_pairs={{0,1},{1,0},{2,3},{3,2},{4,5},{5,4},{6,7},{7,6},{32,65},{33,64},{3... | collective-permute-start | bytes 688136 | tf_op jit(solution)/shard_map/ppermute | solution.py:460
  7.5 4.5 %collective-permute-start.2 = (f32[4,8,128]{2,1,0:T(8,128)S(1)}, f32[4,8,128]{2,1,0:T(8,128)S(1)}, u32[]{:S(2)}, u32[]{:S(2)}) collective-permute-start(f32[4,8,128]{2,1,0:T(8,128)S(1)} %get-tuple-element.47), channel_id=1, source_target_pairs={{1,0},{8,1},{9,8},{16,9},{17,16},{24,17},{25,24},{0,25},{2,3},{11,... | collective-permute-start | bytes 49160 | tf_op jit(solution)/shard_map/ppermute | solution.py:466
  11.9 1.2 %collective-permute-start.3 = (f32[4,8,128]{2,1,0:T(8,128)S(1)}, f32[4,8,128]{2,1,0:T(8,128)S(1)}, u32[]{:S(2)}, u32[]{:S(2)}) collective-permute-start(f32[4,8,128]{2,1,0:T(8,128)S(1)} %get-tuple-element.48), channel_id=1, source_target_pairs={{0,1},{1,8},{8,9},{9,16},{16,17},{17,24},{24,25},{25,0},{3,2},{2,1... | collective-permute-start | bytes 49160 | tf_op jit(solution)/shard_map/ppermute | solution.py:467
  14.7 11.0 %collective-permute-start.8 = (f32[6,8,128]{2,1,0:T(8,128)S(1)}, f32[6,8,128]{2,1,0:T(8,128)S(1)}, u32[]{:S(2)}, u32[]{:S(2)}) collective-permute-start(f32[6,8,128]{2,1,0:T(8,128)S(1)} %get-tuple-element.58), channel_id=1, source_target_pairs={{0,32},{32,0},{64,96},{96,64},{128,160},{160,128},{192,224},{224,1... | collective-permute-start | bytes 73736 | tf_op jit(solution)/shard_map/ppermute | solution.py:474
  18.7 7.0 %collective-permute-start.9 = (f32[6,8,128]{2,1,0:T(8,128)S(1)}, f32[6,8,128]{2,1,0:T(8,128)S(1)}, u32[]{:S(2)}, u32[]{:S(2)}) collective-permute-start(f32[6,8,128]{2,1,0:T(8,128)S(1)} %get-tuple-element.59), channel_id=1, source_target_pairs={{0,0},{32,64},{64,32},{96,128},{128,96},{160,192},{192,160},{224,2... | collective-permute-start | bytes 73736 | tf_op jit(solution)/shard_map/ppermute | solution.py:475
  26.8 6.6 %collective-permute-start.10 = (f32[104,128]{1,0:T(8,128)S(1)}, f32[104,128]{1,0:T(8,128)S(1)}, u32[]{:S(2)}, u32[]{:S(2)}) collective-permute-start(f32[104,128]{1,0:T(8,128)S(1)} %get-tuple-element.64), channel_id=1, source_target_pairs={{0,3},{1,2},{3,0},{2,1},{4,7},{5,6},{7,4},{6,5},{8,11},{9,10},{11,... | collective-permute-start | bytes 159752 | tf_op jit(solution)/shard_map/ppermute | solution.py:484
  33.4 8.2 %collective-permute-start.11 = (f32[104,128]{1,0:T(8,128)S(1)}, f32[104,128]{1,0:T(8,128)S(1)}, u32[]{:S(2)}, u32[]{:S(2)}) collective-permute-start(f32[104,128]{1,0:T(8,128)S(1)} %add.43.a_6_), channel_id=1, source_target_pairs={{0,7},{1,6},{3,4},{2,5},{4,3},{5,2},{7,0},{6,1},{8,15},{9,14},{11,... | collective-permute-start | bytes 159752 | tf_op jit(solution)/shard_map/ppermute | solution.py:485
  44.7 5.8 %collective-permute-start.12 = (f32[96,128]{1,0:T(8,128)S(1)}, f32[96,128]{1,0:T(8,128)S(1)}, u32[]{:S(2)}, u32[]{:S(2)}) collective-permute-start(f32[96,128]{1,0:T(8,128)S(1)} %get-tuple-element.68), channel_id=1, source_target_pairs={{0,7},{1,6},{3,4},{2,5},{4,3},{5,2},{7,0},{6,1},{8,15},{9,14},{11,... | collective-permute-start | bytes 147464 | tf_op jit(solution)/shard_map/ppermute | solution.py:484
  50.6 4.5 %collective-permute-start.13 = (f32[96,128]{1,0:T(8,128)S(1)}, f32[96,128]{1,0:T(8,128)S(1)}, u32[]{:S(2)}, u32[]{:S(2)}) collective-permute-start(f32[96,128]{1,0:T(8,128)S(1)} %add.44.a_6_), channel_id=1, source_target_pairs={{0,3},{1,2},{3,0},{2,1},{4,7},{5,6},{7,4},{6,5},{8,11},{9,10},{11,... | collective-permute-start | bytes 147464 | tf_op jit(solution)/shard_map/ppermute | solution.py:485
  58.0 4.4 %collective-permute-start.14 = (f32[88,128]{1,0:T(8,128)S(1)}, f32[88,128]{1,0:T(8,128)S(1)}, u32[]{:S(2)}, u32[]{:S(2)}) collective-permute-start(f32[88,128]{1,0:T(8,128)S(1)} %get-tuple-element.72), channel_id=1, source_target_pairs={{0,3},{1,2},{3,0},{2,1},{4,7},{5,6},{7,4},{6,5},{8,11},{9,10},{11,... | collective-permute-start | bytes 135176 | tf_op jit(solution)/shard_map/ppermute | solution.py:484
  62.4 6.8 %collective-permute-start.15 = (f32[88,128]{1,0:T(8,128)S(1)}, f32[88,128]{1,0:T(8,128)S(1)}, u32[]{:S(2)}, u32[]{:S(2)}) collective-permute-start(f32[88,128]{1,0:T(8,128)S(1)} %add.45.a_6_), channel_id=1, source_target_pairs={{0,7},{1,6},{3,4},{2,5},{4,3},{5,2},{7,0},{6,1},{8,15},{9,14},{11,... | collective-permute-start | bytes 135176 | tf_op jit(solution)/shard_map/ppermute | solution.py:485
  71.9 6.0 %collective-permute-start.16 = (f32[80,128]{1,0:T(8,128)S(1)}, f32[80,128]{1,0:T(8,128)S(1)}, u32[]{:S(2)}, u32[]{:S(2)}) collective-permute-start(f32[80,128]{1,0:T(8,128)S(1)} %get-tuple-element.76), channel_id=1, source_target_pairs={{0,7},{1,6},{3,4},{2,5},{4,3},{5,2},{7,0},{6,1},{8,15},{9,14},{11,... | collective-permute-start | bytes 122888 | tf_op jit(solution)/shard_map/ppermute | solution.py:484
  77.9 4.3 %collective-permute-start.17 = (f32[80,128]{1,0:T(8,128)S(1)}, f32[80,128]{1,0:T(8,128)S(1)}, u32[]{:S(2)}, u32[]{:S(2)}) collective-permute-start(f32[80,128]{1,0:T(8,128)S(1)} %add.46.a_4_), channel_id=1, source_target_pairs={{0,3},{1,2},{3,0},{2,1},{4,7},{5,6},{7,4},{6,5},{8,11},{9,10},{11,... | collective-permute-start | bytes 122888 | tf_op jit(solution)/shard_map/ppermute | solution.py:485
  83.3 2.6 %collective-permute-start.18 = (f32[2,4,28,8,128]{4,3,2,1,0:T(8,128)S(1)}, f32[2,4,28,8,128]{4,3,2,1,0:T(8,128)S(1)}, u32[]{:S(2)}, u32[]{:S(2)}) collective-permute-start(f32[2,4,28,8,128]{4,3,2,1,0:T(8,128)S(1)} %shard_map.39), channel_id=1, source_target_pairs={{0,1},{1,0},{2,3},{3,2},{4,5},{5,4},{6,7},{7,6},{8,9},{9,8},{10,11... | collective-permute-start | bytes 2752520 | tf_op jit(solution)/shard_map/ppermute | solution.py:496

commit v2 on v1

--- a/solution.py
+++ b/solution.py
@@ -91,7 +91,7 @@
     return copies
 
 
-def split(z, facing_b, place, noisy, edge, *refs):
+def split(z, facing_b, place, noisy, *refs):
     weights, (keep, send, msg_keep, msg_send), more = refs[0], refs[facing_b : facing_b + 4], refs[facing_b + 4 :]
     sem_k, sem_s = more[facing_b : facing_b + 2]
     half, odd = place[1], place[2]
@@ -127,7 +127,7 @@
         rows(send, 8 - M, msg_send)
 
 
-def assemble(z, place, keep_a, send_a, keep_b, send_b, w, edge, ne, col_l, col_r):
+def assemble(z, place, keep_a, send_a, keep_b, send_b, w, ne, col_l, col_r):
     core, odd = place[0], place[2]
     q4 = z.rest
     for keep, recv, group in ((keep_a, send_a, 1 - odd), (keep_b, send_b, odd)):
@@ -154,7 +154,7 @@
         col_r[v] = tile
 
 
-def frame_cols(z, place, ne_in, w, edge, from_r, from_l, ne, wx, qx, qy, sums, cor_a, cor_b, acc):
+def frame_cols(z, place, ne_in, w, from_r, from_l, ne, wx, qx, qy, sums, cor_a, cor_b, acc):
     lane = lane_iota((8, LANES))
     per = LANES // M
     units = z.r * z.bt + z.r // 8
@@ -183,11 +183,11 @@
         cor_a[v] = jnp.where(odd == 0, d, u)
         cor_b[v] = jnp.where(odd == 0, u, d)
     sums[...] = jnp.zeros_like(sums)
-    first_q(z, ne, edge, [(M, M + z.r - 1)], qx, qy, acc, sums)
-
-
-def first_q(z, ne, edge, runs, qx, qy, acc, sums):
-    across, along = masks(z, edge)
+    first_q(z, ne, [(M, M + z.r - 1)], qx, qy, acc, sums)
+
+
+def first_q(z, ne, runs, qx, qy, acc, sums):
+    across, along = masks(z)
     acc[...] = jnp.zeros_like(acc)
 
     def band_tile(t, _):
@@ -209,10 +209,16 @@
             sums[e : e + 1, :] = jnp.sum(acc[e], axis=0, keepdims=True)
 
 
-def masks(z, edge):
-    rows = {M - 1: edge[0:1, :], M + z.r - 1: edge[1:2, :]}
+def masks(z):
+    row, half = lax.axis_index("row"), here()[1]
+    rows = {
+        M - 1: jnp.where(row > 0, 1.0, 0.0),
+        M + z.r - 1: jnp.where(row < lax.axis_size("row") - 1, 1.0, 0.0),
+    }
     cut = z.c - LANES
-    tail = jnp.broadcast_to(edge[2:3, cut : z.ec], (8, z.ec - cut))
+    lane = lane_iota((8, z.ec - cut)) + cut
+    col = lax.axis_index("col") * (2 * z.c) + half * z.c + jnp.where(lane < z.c + LANES // 2, lane, lane - z.ec)
+    tail = jnp.where((col >= 0) & (col < lax.axis_size("col") * (2 * z.c) - 1), 1.0, 0.0)
 
     def across(e, d):
         return d * rows[e] if e in rows else d
@@ -266,7 +272,7 @@
         scale[e] = jnp.broadcast_to(sums[e : e + 1, :], (8, z.ec))
 
 
-def frame_rows(z, place, ne_in, qx_in, qy_in, wx_in, sums_in, edge, a_keep, a_send, b_keep, b_send, cor_a, cor_b, ne, qx, qy, wx, msg, acc, sums):
+def frame_rows(z, place, ne_in, qx_in, qy_in, wx_in, sums_in, a_keep, a_send, b_keep, b_send, cor_a, cor_b, ne, qx, qy, wx, msg, acc, sums):
     core, odd = place[0], place[2]
     lane = lane_iota((8, LANES))
     sub = lax.broadcasted_iota(jnp.int32, (8, z.c), 0)
@@ -308,7 +314,7 @@
     wx[M + z.r : z.er, z.c : z.ec] = corner(below, M * z.bt)[0:M]
     wx[0:M, z.c : z.ec] = corner(above, M * z.bt)[8 - M : 8]
     sums[...] = sums_in[...]
-    first_q(z, ne, edge, [(0, M), (M + z.r - 1, z.er - 1)], qx, qy, acc, sums)
+    first_q(z, ne, [(0, M), (M + z.r - 1, z.er - 1)], qx, qy, acc, sums)
     pack_message(z, 0, sums, msg)
 
 
@@ -325,11 +331,11 @@
     lax.fori_loop(0, z.bt, band_tile, 0)
 
 
-def step(z, k, base, wx, edge, u_in, qx_in, qy_in, msg_a, msg_b, u, qx, qy, msg, sums, scale, acc, ubs, pxs, pys):
+def step(z, k, base, wx, u_in, qx_in, qy_in, msg_a, msg_b, u, qx, qy, msg, sums, scale, acc, ubs, pxs, pys):
     lo, hi = k, z.er - 1 - k
     read_scale(z, k, msg_a, msg_b, wx, sums, scale)
     acc[...] = jnp.zeros_like(acc)
-    across, along = masks(z, edge)
+    across, along = masks(z)
 
     def band_tile(t, _):
         px0 = scale[lo] * qx_in[QX0 + lo, t]
@@ -407,16 +413,6 @@
     z = Sizes(*noisy.shape)
     n_row, n_col, n_band = (lax.axis_size(a) for a in ("row", "col", "band"))
     chips = n_band // 2
-    _, half, _ = here()
-    row0 = lax.axis_index("row") * z.r
-    col0 = lax.axis_index("col") * (2 * z.c) + half * z.c
-
-    lane = jnp.arange(z.ec)
-    gcol = col0 + jnp.where(lane < z.c + LANES // 2, lane, lane - z.ec)
-    inner = (gcol >= 0) & (gcol < n_col * 2 * z.c - 1)
-    edge = jnp.stack([
-        jnp.broadcast_to(row0 > 0, (z.ec,)), jnp.broadcast_to(row0 + z.r < n_row * z.r, (z.ec,)), inner,
-    ] + [inner] * 5).astype(F32)
 
     def at(chip, h):
         return 2 * chip + (h ^ (chip % 2))
@@ -432,7 +428,6 @@
     to_right = [(line[j], line[(j + 1) % len(line)]) for line in spot for j in range(len(line))]
     to_left = [(b, a) for a, b in to_right]
 
-    (edge,) = lax.optimization_barrier((edge,))
 
     units = z.r * z.bt + z.r // 8
     n_edge = -(-units // (LANES // M))
@@ -453,15 +448,15 @@
         b = name == "b"
         keep, send, msg_keep, msg_send, *w = call(
             lambda *a, b=b: split(z, b, here(), *a), [block, block, bulk, bulk] + [(z.r, z.c)] * b,
-            [cube, edge] + [weights] * b, scratch=[sem_g, sem_g] + [pltpu.SemaphoreType.DMA] * b,
-            hbm_in=(0, 2), flops=cost,
+            [cube] + [weights] * b, scratch=[sem_g, sem_g] + [pltpu.SemaphoreType.DMA] * b,
+            hbm_in=(0, 1), flops=cost,
         )
         far.append(lax.ppermute(msg_keep, "row", same))
         far.append(lax.ppermute(msg_send, ("row", "band"), cross))
         parts += [keep, lax.ppermute(send, "band", swap)]
     (w,) = w
     ne, col_l, col_r = call(
-        lambda *a: assemble(z, here(), *a), [state, side, side], [*parts, w, edge], flops=cost
+        lambda *a: assemble(z, here(), *a), [state, side, side], [*parts, w], flops=cost
     )
     from_r = lax.ppermute(col_l, ("col", "band"), to_left)
     from_l = lax.ppermute(col_r, ("col", "band"), to_right)
@@ -469,13 +464,13 @@
     one = pltpu.VMEM(flat, F32)
     ne, wx, qx, qy, sums, cor_a, cor_b = call(
         lambda *a: frame_cols(z, here(), *a), [state, flat, state, state, flat, corner, corner],
-        [ne, w, edge, from_r, from_l], aliases={0: 0}, scratch=[acc], flops=5 * cost,
+        [ne, w, from_r, from_l], aliases={0: 0}, scratch=[acc], flops=5 * cost,
     )
     cor_a = lax.ppermute(cor_a, "row", rows_a)
     cor_b = lax.ppermute(cor_b, "row", rows_b)
     ne, qx, qy, wx, msg = call(
         lambda *a: frame_rows(z, here(), *a), [state, state, state, flat, message_shape(z, 0)],
-        [ne, qx, qy, wx, sums, edge, *far, cor_a, cor_b],
+        [ne, qx, qy, wx, sums, *far, cor_a, cor_b],
         aliases={0: 0, 1: 1, 2: 2}, scratch=[acc, one], flops=5 * cost,
     )
     u = base = ne
@@ -488,7 +483,7 @@
         if k < ITERS - 1:
             u, qx, qy, msg = call(
                 lambda *a, k=k: step(z, k, *a), [state, state, state, message_shape(z, k + 1)],
-                [base, wx, edge, u, qx, qy, msg, other], scratch=[one, acc, acc, acc, acc, acc], flops=20 * cost,
+                [base, wx, u, qx, qy, msg, other], scratch=[one, acc, acc, acc, acc, acc], flops=20 * cost,
             )
     last = [base, wx, qx, qy, msg, other]
     room = [one, acc, pltpu.VMEM((z.r, z.ft + 1, 8, z.c), F32)]

time: 88.3 us -> 88.1 us (level)
  no operation moved by 1% of the time
where the time goes in v2:
time: 88.1 us; the launch traced here: 86.7 us
  waiting for transfers between devices  35.8 us (41%)
  starting transfers between devices  30.5 us (35%)
  Pallas kernels  20.1 us (23%)
    pallas_call x15, Pallas kernels, call(): pl.pallas_call(body, out_shape=[(pltpu.HBM if i in hbm_out else pltpu.VME...  20.1 us
    ppermute x4, waiting for transfers between devices, local(): other = lax.ppermute(msg, 'band', pairs[1])  12.3 us
    ppermute x4, waiting for transfers between devices, local(): msg = msg + lax.ppermute(msg, 'band', pairs[0])  11.7 us
    ppermute x4, starting transfers between devices, local(): msg = msg + lax.ppermute(msg, 'band', pairs[0])  11.2 us
    ppermute x4, starting transfers between devices, local(): other = lax.ppermute(msg, 'band', pairs[1])  10.3 us
    ppermute x1, waiting for transfers between devices, local(): cor_a = lax.ppermute(cor_a, 'row', rows_a)  6.33 us
    ppermute x1, starting transfers between devices, local(): cor_a = lax.ppermute(cor_a, 'row', rows_a)  3.95 us
    ppermute x1, waiting for transfers between devices, local(): from_r = lax.ppermute(col_l, ('col', 'band'), to_left)  3.88 us
  transfers between devices with their start and end apart: 19, of which 12 were waited for; matrix products, arithmetic and copies ran while one was open for 0% of the time, Pallas kernels for 8%

profile of v2, /device:TPU:63, one launch (start us, length us, event | category | flops | bytes accessed | tf_op | source)
XLA Modules:
  0.0 86.7 jit_solution(5382730456622487071)
XLA Ops:
  0.0 1.4 %shard_map.28 = (f32[4,28,8,128]{3,2,1,0:T(8,128)S(1)}, f32[4,28,8,128]{3,2,1,0:T(8,128)S(1)}, f32[14,8,512]{2,1,0:T(8,128)S(1)}, f32[14,8,512]{2,1,0:T(8,128)S(1)}) custom-call(f32[28,16,1024]{2,1,0:T(8,128)} %a_0_.3), custom_call_target="tpu_custom_call" | custom-call | flops 860160 | tf_op jit(solution)/shard_map/pallas_call | solution.py:26
  2.2 1.4 %shard_map.29 = (f32[4,28,8,128]{3,2,1,0:T(8,128)S(1)}, f32[4,28,8,128]{3,2,1,0:T(8,128)S(1)}, f32[14,8,512]{2,1,0:T(8,128)S(1)}, f32[14,8,512]{2,1,0:T(8,128)S(1)}, f32[16,512]{1,0:T(8,128)S(1)}) custom-call(f32[28,16,1024]{2,1,0:T(8,128)} %a_0_.3, f32[16,1024]{1,0:T(8,128)} %a_1_.1), custom_call_target="tpu_custom_call" | custom-call | flops 860160 | tf_op jit(solution)/shard_map/pallas_call | solution.py:26
  3.8 2.0 %collective-permute-start.5 = (f32[14,8,512]{2,1,0:T(8,128)S(1)}, f32[14,8,512]{2,1,0:T(8,128)S(1)}, u32[]{:S(2)}, u32[]{:S(2)}) collective-permute-start(f32[14,8,512]{2,1,0:T(8,128)S(1)} %get-tuple-element.55), channel_id=1, source_target_pairs={{0,33},{1,32},{2,35},{3,34},{4,37},{5,36},{6,39},{7,38},{32,1},{33... | collective-permute-start | bytes 688136 | tf_op jit(solution)/shard_map/ppermute | solution.py:455
  7.9 3.9 %collective-permute-done.2.a_2_ = f32[4,8,128]{2,1,0:T(8,128)S(1)} collective-permute-done((f32[4,8,128]{2,1,0:T(8,128)S(1)}, f32[4,8,128]{2,1,0:T(8,128)S(1)}, u32[]{:S(2)}, u32[]{:S(2)}) %collective-permute-start.2) | collective-permute-done | bytes 16416 | tf_op jit(solution)/shard_map/ppermute | solution.py:461
  11.8 1.2 %collective-permute-done.3.a_3_ = f32[4,8,128]{2,1,0:T(8,128)S(1)} collective-permute-done((f32[4,8,128]{2,1,0:T(8,128)S(1)}, f32[4,8,128]{2,1,0:T(8,128)S(1)}, u32[]{:S(2)}, u32[]{:S(2)}) %collective-permute-start.3) | collective-permute-done | bytes 16416 | tf_op jit(solution)/shard_map/ppermute | solution.py:462
  13.0 1.6 %shard_map.31 = (f32[28,7,8,640]{3,2,1,0:T(8,128)S(1)}, f32[24,640]{1,0:T(8,128)S(1)}, f32[28,7,8,640]{3,2,1,0:T(8,128)S(1)}, f32[28,7,8,640]{3,2,1,0:T(8,128)S(...) custom-call(f32[28,7,8,640]{3,2,1,0:T(8,128)S(1)} %get-tuple-element, ...), custom_call_target="tpu_custom_call", output_to_operand_aliasing={{0}: (0, {})} | custom-call | flops 4300800 | tf_op jit(solution)/shard_map/pallas_call | solution.py:26
  14.6 3.9 %collective-permute-start.8 = (f32[6,8,128]{2,1,0:T(8,128)S(1)}, f32[6,8,128]{2,1,0:T(8,128)S(1)}, u32[]{:S(2)}, u32[]{:S(2)}) collective-permute-start(f32[6,8,128]{2,1,0:T(8,128)S(1)} %get-tuple-element.58), channel_id=1, source_target_pairs={{0,32},{32,0},{64,96},{96,64},{128,160},{160,128},{192,224},{224,1... | collective-permute-start | bytes 73736 | tf_op jit(solution)/shard_map/ppermute | solution.py:469
  19.2 6.3 %collective-permute-done.8.a_9_ = f32[6,8,128]{2,1,0:T(8,128)S(1)} collective-permute-done((f32[6,8,128]{2,1,0:T(8,128)S(1)}, f32[6,8,128]{2,1,0:T(8,128)S(1)}, u32[]{:S(2)}, u32[]{:S(2)}) %collective-permute-start.8) | collective-permute-done | bytes 24608 | tf_op jit(solution)/shard_map/ppermute | solution.py:469
  26.7 4.7 %collective-permute-start.10 = (f32[104,128]{1,0:T(8,128)S(1)}, f32[104,128]{1,0:T(8,128)S(1)}, u32[]{:S(2)}, u32[]{:S(2)}) collective-permute-start(f32[104,128]{1,0:T(8,128)S(1)} %get-tuple-element.64), channel_id=1, source_target_pairs={{0,3},{1,2},{3,0},{2,1},{4,7},{5,6},{7,4},{6,5},{8,11},{9,10},{11,... | collective-permute-start | bytes 159752 | tf_op jit(solution)/shard_map/ppermute | solution.py:479
  31.4 1.9 %collective-permute-done.10 = f32[104,128]{1,0:T(8,128)S(1)} collective-permute-done((f32[104,128]{1,0:T(8,128)S(1)}, f32[104,128]{1,0:T(8,128)S(1)}, u32[]{:S(2)}, u32[]{:S(2)}) %collective-permute-start.10) | collective-permute-done | bytes 53280 | tf_op jit(solution)/shard_map/ppermute | solution.py:479
  33.3 6.0 %collective-permute-start.11 = (f32[104,128]{1,0:T(8,128)S(1)}, f32[104,128]{1,0:T(8,128)S(1)}, u32[]{:S(2)}, u32[]{:S(2)}) collective-permute-start(f32[104,128]{1,0:T(8,128)S(1)} %add.12.a_5_), channel_id=1, source_target_pairs={{0,7},{1,6},{3,4},{2,5},{4,3},{5,2},{7,0},{6,1},{8,15},{9,14},{11,... | collective-permute-start | bytes 159752 | tf_op jit(solution)/shard_map/ppermute | solution.py:480
  39.2 2.3 %collective-permute-done.11.a_6_ = f32[104,128]{1,0:T(8,128)S(1)} collective-permute-done((f32[104,128]{1,0:T(8,128)S(1)}, f32[104,128]{1,0:T(8,128)S(1)}, u32[]{:S(2)}, u32[]{:S(2)}) %collective-permute-start.11) | collective-permute-done | bytes 53280 | tf_op jit(solution)/shard_map/ppermute | solution.py:480
  41.5 3.0 %shard_map.33 = (f32[28,7,8,640]{3,2,1,0:T(8,128)S(1)}, f32[28,7,8,640]{3,2,1,0:T(8,128)S(1)}, f32[28,7,8,640]{3,2,1,0:T(8,128)S(1)}, f32[96,128]{1,0:T(8,128)S(1)}) custom-call(f32[28,7,8,640]{3,2,1,0:T(8,128)S(1)} %get-tuple-element.60.a_0_.a_2_, f32[24,640]{1,0:T(8,128)S(1)} %get-tuple-element.61.a_1_, f32[28,7,8,640]{3,2,1,0:T(8,128)S(1)} %get-tuple-element.60.a_0_.a_2_, ...), custom_call_target="tpu_custom_call" | custom-call | flops 17203200 | tf_op jit(solution)/shard_map/pallas_call | solution.py:26
  44.5 3.4 %collective-permute-start.12 = (f32[96,128]{1,0:T(8,128)S(1)}, f32[96,128]{1,0:T(8,128)S(1)}, u32[]{:S(2)}, u32[]{:S(2)}) collective-permute-start(f32[96,128]{1,0:T(8,128)S(1)} %get-tuple-element.68), channel_id=1, source_target_pairs={{0,7},{1,6},{3,4},{2,5},{4,3},{5,2},{7,0},{6,1},{8,15},{9,14},{11,... | collective-permute-start | bytes 147464 | tf_op jit(solution)/shard_map/ppermute | solution.py:479
  47.9 2.4 %collective-permute-done.12 = f32[96,128]{1,0:T(8,128)S(1)} collective-permute-done((f32[96,128]{1,0:T(8,128)S(1)}, f32[96,128]{1,0:T(8,128)S(1)}, u32[]{:S(2)}, u32[]{:S(2)}) %collective-permute-start.12) | collective-permute-done | bytes 49184 | tf_op jit(solution)/shard_map/ppermute | solution.py:479
  51.6 3.2 %collective-permute-done.13.a_6_ = f32[96,128]{1,0:T(8,128)S(1)} collective-permute-done((f32[96,128]{1,0:T(8,128)S(1)}, f32[96,128]{1,0:T(8,128)S(1)}, u32[]{:S(2)}, u32[]{:S(2)}) %collective-permute-start.13) | collective-permute-done | bytes 49184 | tf_op jit(solution)/shard_map/ppermute | solution.py:480
  54.9 2.9 %shard_map.35 = (f32[28,7,8,640]{3,2,1,0:T(8,128)S(1)}, f32[28,7,8,640]{3,2,1,0:T(8,128)S(1)}, f32[28,7,8,640]{3,2,1,0:T(8,128)S(1)}, f32[88,128]{1,0:T(8,128)S(1)}) custom-call(f32[28,7,8,640]{3,2,1,0:T(8,128)S(1)} %shard_map.34.a_0_, f32[24,640]{1,0:T(8,128)S(1)} %get-tuple-element.61.a_1_, f32[28,7,8,640]{3,2,1,0:T(8,128)S(1)} %get-tuple-element.65.a_1_.a_2_, ...), custom_call_target="tpu_custom_call" | custom-call | flops 17203200 | tf_op jit(solution)/shard_map/pallas_call | solution.py:26
  58.5 3.7 %collective-permute-done.14 = f32[88,128]{1,0:T(8,128)S(1)} collective-permute-done((f32[88,128]{1,0:T(8,128)S(1)}, f32[88,128]{1,0:T(8,128)S(1)}, u32[]{:S(2)}, u32[]{:S(2)}) %collective-permute-start.14) | collective-permute-done | bytes 45088 | tf_op jit(solution)/shard_map/ppermute | solution.py:479
  62.1 3.5 %collective-permute-start.15 = (f32[88,128]{1,0:T(8,128)S(1)}, f32[88,128]{1,0:T(8,128)S(1)}, u32[]{:S(2)}, u32[]{:S(2)}) collective-permute-start(f32[88,128]{1,0:T(8,128)S(1)} %add.14.a_5_), channel_id=1, source_target_pairs={{0,7},{1,6},{3,4},{2,5},{4,3},{5,2},{7,0},{6,1},{8,15},{9,14},{11,... | collective-permute-start | bytes 135176 | tf_op jit(solution)/shard_map/ppermute | solution.py:480
  66.1 2.8 %collective-permute-done.15.a_6_ = f32[88,128]{1,0:T(8,128)S(1)} collective-permute-done((f32[88,128]{1,0:T(8,128)S(1)}, f32[88,128]{1,0:T(8,128)S(1)}, u32[]{:S(2)}, u32[]{:S(2)}) %collective-permute-start.15) | collective-permute-done | bytes 45088 | tf_op jit(solution)/shard_map/ppermute | solution.py:480
  69.0 2.7 %shard_map.37 = (f32[28,7,8,640]{3,2,1,0:T(8,128)S(1)}, f32[28,7,8,640]{3,2,1,0:T(8,128)S(1)}, f32[28,7,8,640]{3,2,1,0:T(8,128)S(1)}, f32[80,128]{1,0:T(8,128)S(1)}) custom-call(f32[28,7,8,640]{3,2,1,0:T(8,128)S(1)} %shard_map.36.a_0_, f32[24,640]{1,0:T(8,128)S(1)} %get-tuple-element.61.a_1_, f32[28,7,8,640]{3,2,1,0:T(8,128)S(1)} %get-tuple-element.69.a_1_.a_2_, ...), custom_call_target="tpu_custom_call" | custom-call | flops 17203200 | tf_op jit(solution)/shard_map/pallas_call | solution.py:26
  71.6 2.3 %collective-permute-start.16 = (f32[80,128]{1,0:T(8,128)S(1)}, f32[80,128]{1,0:T(8,128)S(1)}, u32[]{:S(2)}, u32[]{:S(2)}) collective-permute-start(f32[80,128]{1,0:T(8,128)S(1)} %get-tuple-element.76), channel_id=1, source_target_pairs={{0,7},{1,6},{3,4},{2,5},{4,3},{5,2},{7,0},{6,1},{8,15},{9,14},{11,... | collective-permute-start | bytes 122888 | tf_op jit(solution)/shard_map/ppermute | solution.py:479
  74.0 3.7 %collective-permute-done.16 = f32[80,128]{1,0:T(8,128)S(1)} collective-permute-done((f32[80,128]{1,0:T(8,128)S(1)}, f32[80,128]{1,0:T(8,128)S(1)}, u32[]{:S(2)}, u32[]{:S(2)}) %collective-permute-start.16) | collective-permute-done | bytes 40992 | tf_op jit(solution)/shard_map/ppermute | solution.py:479
  78.1 3.9 %collective-permute-done.17.a_5_ = f32[80,128]{1,0:T(8,128)S(1)} collective-permute-done((f32[80,128]{1,0:T(8,128)S(1)}, f32[80,128]{1,0:T(8,128)S(1)}, u32[]{:S(2)}, u32[]{:S(2)}) %collective-permute-start.17) | collective-permute-done | bytes 40992 | tf_op jit(solution)/shard_map/ppermute | solution.py:480
  (33 shorter events, 12.1 us)
Async XLA Ops:
  1.4 5.1 %collective-permute-start = (f32[4,28,8,128]{3,2,1,0:T(8,128)S(1)}, f32[4,28,8,128]{3,2,1,0:T(8,128)S(1)}, u32[]{:S(2)}, u32[]{:S(2)}) collective-permute-start(f32[4,28,8,128]{3,2,1,0:T(8,128)S(1)} %get-tuple-element.42), channel_id=1, source_target_pairs={{0,1},{1,0},{2,3},{3,2},{4,5},{5,4},{6,7},{7,6},{8,9},{9,8},{10,11... | collective-permute-start | bytes 1376264 | tf_op jit(solution)/shard_map/ppermute | solution.py:456
  3.6 3.0 %collective-permute-start.1 = (f32[4,28,8,128]{3,2,1,0:T(8,128)S(1)}, f32[4,28,8,128]{3,2,1,0:T(8,128)S(1)}, u32[]{:S(2)}, u32[]{:S(2)}) collective-permute-start(f32[4,28,8,128]{3,2,1,0:T(8,128)S(1)} %get-tuple-element.44), channel_id=1, source_target_pairs={{0,1},{1,0},{2,3},{3,2},{4,5},{5,4},{6,7},{7,6},{8,9},{9,8},{10,11... | collective-permute-start | bytes 1376264 | tf_op jit(solution)/shard_map/ppermute | solution.py:456
  3.8 14.8 %collective-permute-start.4 = (f32[14,8,512]{2,1,0:T(8,128)S(1)}, f32[14,8,512]{2,1,0:T(8,128)S(1)}, u32[]{:S(2)}, u32[]{:S(2)}) collective-permute-start(f32[14,8,512]{2,1,0:T(8,128)S(1)} %get-tuple-element.54), channel_id=1, source_target_pairs={{0,32},{32,0},{64,96},{96,64},{128,160},{160,128},{192,224},{224,1... | collective-permute-start | bytes 688136 | tf_op jit(solution)/shard_map/ppermute | solution.py:454
  3.8 15.4 %collective-permute-start.5 = (f32[14,8,512]{2,1,0:T(8,128)S(1)}, f32[14,8,512]{2,1,0:T(8,128)S(1)}, u32[]{:S(2)}, u32[]{:S(2)}) collective-permute-start(f32[14,8,512]{2,1,0:T(8,128)S(1)} %get-tuple-element.55), channel_id=1, source_target_pairs={{0,33},{1,32},{2,35},{3,34},{4,37},{5,36},{6,39},{7,38},{32,1},{33... | collective-permute-start | bytes 688136 | tf_op jit(solution)/shard_map/ppermute | solution.py:455
  5.9 13.3 %collective-permute-start.6 = (f32[14,8,512]{2,1,0:T(8,128)S(1)}, f32[14,8,512]{2,1,0:T(8,128)S(1)}, u32[]{:S(2)}, u32[]{:S(2)}) collective-permute-start(f32[14,8,512]{2,1,0:T(8,128)S(1)} %get-tuple-element.56), channel_id=1, source_target_pairs={{0,0},{32,64},{64,32},{96,128},{128,96},{160,192},{192,160},{224,2... | collective-permute-start | bytes 688136 | tf_op jit(solution)/shard_map/ppermute | solution.py:454
  6.5 12.7 %collective-permute-start.7 = (f32[14,8,512]{2,1,0:T(8,128)S(1)}, f32[14,8,512]{2,1,0:T(8,128)S(1)}, u32[]{:S(2)}, u32[]{:S(2)}) collective-permute-start(f32[14,8,512]{2,1,0:T(8,128)S(1)} %get-tuple-element.57), channel_id=1, source_target_pairs={{0,1},{1,0},{2,3},{3,2},{4,5},{5,4},{6,7},{7,6},{32,65},{33,64},{3... | collective-permute-start | bytes 688136 | tf_op jit(solution)/shard_map/ppermute | solution.py:455
  7.3 4.5 %collective-permute-start.2 = (f32[4,8,128]{2,1,0:T(8,128)S(1)}, f32[4,8,128]{2,1,0:T(8,128)S(1)}, u32[]{:S(2)}, u32[]{:S(2)}) collective-permute-start(f32[4,8,128]{2,1,0:T(8,128)S(1)} %get-tuple-element.47), channel_id=1, source_target_pairs={{1,0},{8,1},{9,8},{16,9},{17,16},{24,17},{25,24},{0,25},{2,3},{11,... | collective-permute-start | bytes 49160 | tf_op jit(solution)/shard_map/ppermute | solution.py:461
  11.8 1.2 %collective-permute-start.3 = (f32[4,8,128]{2,1,0:T(8,128)S(1)}, f32[4,8,128]{2,1,0:T(8,128)S(1)}, u32[]{:S(2)}, u32[]{:S(2)}) collective-permute-start(f32[4,8,128]{2,1,0:T(8,128)S(1)} %get-tuple-element.48), channel_id=1, source_target_pairs={{0,1},{1,8},{8,9},{9,16},{16,17},{17,24},{24,25},{25,0},{3,2},{2,1... | collective-permute-start | bytes 49160 | tf_op jit(solution)/shard_map/ppermute | solution.py:462
  14.6 11.0 %collective-permute-start.8 = (f32[6,8,128]{2,1,0:T(8,128)S(1)}, f32[6,8,128]{2,1,0:T(8,128)S(1)}, u32[]{:S(2)}, u32[]{:S(2)}) collective-permute-start(f32[6,8,128]{2,1,0:T(8,128)S(1)} %get-tuple-element.58), channel_id=1, source_target_pairs={{0,32},{32,0},{64,96},{96,64},{128,160},{160,128},{192,224},{224,1... | collective-permute-start | bytes 73736 | tf_op jit(solution)/shard_map/ppermute | solution.py:469
  18.5 7.0 %collective-permute-start.9 = (f32[6,8,128]{2,1,0:T(8,128)S(1)}, f32[6,8,128]{2,1,0:T(8,128)S(1)}, u32[]{:S(2)}, u32[]{:S(2)}) collective-permute-start(f32[6,8,128]{2,1,0:T(8,128)S(1)} %get-tuple-element.59), channel_id=1, source_target_pairs={{0,0},{32,64},{64,32},{96,128},{128,96},{160,192},{192,160},{224,2... | collective-permute-start | bytes 73736 | tf_op jit(solution)/shard_map/ppermute | solution.py:470
  26.7 6.6 %collective-permute-start.10 = (f32[104,128]{1,0:T(8,128)S(1)}, f32[104,128]{1,0:T(8,128)S(1)}, u32[]{:S(2)}, u32[]{:S(2)}) collective-permute-start(f32[104,128]{1,0:T(8,128)S(1)} %get-tuple-element.64), channel_id=1, source_target_pairs={{0,3},{1,2},{3,0},{2,1},{4,7},{5,6},{7,4},{6,5},{8,11},{9,10},{11,... | collective-permute-start | bytes 159752 | tf_op jit(solution)/shard_map/ppermute | solution.py:479
  33.3 8.2 %collective-permute-start.11 = (f32[104,128]{1,0:T(8,128)S(1)}, f32[104,128]{1,0:T(8,128)S(1)}, u32[]{:S(2)}, u32[]{:S(2)}) collective-permute-start(f32[104,128]{1,0:T(8,128)S(1)} %add.12.a_5_), channel_id=1, source_target_pairs={{0,7},{1,6},{3,4},{2,5},{4,3},{5,2},{7,0},{6,1},{8,15},{9,14},{11,... | collective-permute-start | bytes 159752 | tf_op jit(solution)/shard_map/ppermute | solution.py:480
  44.5 5.8 %collective-permute-start.12 = (f32[96,128]{1,0:T(8,128)S(1)}, f32[96,128]{1,0:T(8,128)S(1)}, u32[]{:S(2)}, u32[]{:S(2)}) collective-permute-start(f32[96,128]{1,0:T(8,128)S(1)} %get-tuple-element.68), channel_id=1, source_target_pairs={{0,7},{1,6},{3,4},{2,5},{4,3},{5,2},{7,0},{6,1},{8,15},{9,14},{11,... | collective-permute-start | bytes 147464 | tf_op jit(solution)/shard_map/ppermute | solution.py:479
  50.4 4.5 %collective-permute-start.13 = (f32[96,128]{1,0:T(8,128)S(1)}, f32[96,128]{1,0:T(8,128)S(1)}, u32[]{:S(2)}, u32[]{:S(2)}) collective-permute-start(f32[96,128]{1,0:T(8,128)S(1)} %add.13.a_5_), channel_id=1, source_target_pairs={{0,3},{1,2},{3,0},{2,1},{4,7},{5,6},{7,4},{6,5},{8,11},{9,10},{11,... | collective-permute-start | bytes 147464 | tf_op jit(solution)/shard_map/ppermute | solution.py:480
  57.7 4.4 %collective-permute-start.14 = (f32[88,128]{1,0:T(8,128)S(1)}, f32[88,128]{1,0:T(8,128)S(1)}, u32[]{:S(2)}, u32[]{:S(2)}) collective-permute-start(f32[88,128]{1,0:T(8,128)S(1)} %get-tuple-element.72), channel_id=1, source_target_pairs={{0,3},{1,2},{3,0},{2,1},{4,7},{5,6},{7,4},{6,5},{8,11},{9,10},{11,... | collective-permute-start | bytes 135176 | tf_op jit(solution)/shard_map/ppermute | solution.py:479
  62.1 6.8 %collective-permute-start.15 = (f32[88,128]{1,0:T(8,128)S(1)}, f32[88,128]{1,0:T(8,128)S(1)}, u32[]{:S(2)}, u32[]{:S(2)}) collective-permute-start(f32[88,128]{1,0:T(8,128)S(1)} %add.14.a_5_), channel_id=1, source_target_pairs={{0,7},{1,6},{3,4},{2,5},{4,3},{5,2},{7,0},{6,1},{8,15},{9,14},{11,... | collective-permute-start | bytes 135176 | tf_op jit(solution)/shard_map/ppermute | solution.py:480
  71.6 6.0 %collective-permute-start.16 = (f32[80,128]{1,0:T(8,128)S(1)}, f32[80,128]{1,0:T(8,128)S(1)}, u32[]{:S(2)}, u32[]{:S(2)}) collective-permute-start(f32[80,128]{1,0:T(8,128)S(1)} %get-tuple-element.76), channel_id=1, source_target_pairs={{0,7},{1,6},{3,4},{2,5},{4,3},{5,2},{7,0},{6,1},{8,15},{9,14},{11,... | collective-permute-start | bytes 122888 | tf_op jit(solution)/shard_map/ppermute | solution.py:479
  77.7 4.3 %collective-permute-start.17 = (f32[80,128]{1,0:T(8,128)S(1)}, f32[80,128]{1,0:T(8,128)S(1)}, u32[]{:S(2)}, u32[]{:S(2)}) collective-permute-start(f32[80,128]{1,0:T(8,128)S(1)} %add.15.a_4_), channel_id=1, source_target_pairs={{0,3},{1,2},{3,0},{2,1},{4,7},{5,6},{7,4},{6,5},{8,11},{9,10},{11,... | collective-permute-start | bytes 122888 | tf_op jit(solution)/shard_map/ppermute | solution.py:480
  83.0 2.6 %collective-permute-start.18 = (f32[2,4,28,8,128]{4,3,2,1,0:T(8,128)S(1)}, f32[2,4,28,8,128]{4,3,2,1,0:T(8,128)S(1)}, u32[]{:S(2)}, u32[]{:S(2)}) collective-permute-start(f32[2,4,28,8,128]{4,3,2,1,0:T(8,128)S(1)} %shard_map.39), channel_id=1, source_target_pairs={{0,1},{1,0},{2,3},{3,2},{4,5},{5,4},{6,7},{7,6},{8,9},{9,8},{10,11... | collective-permute-start | bytes 2752520 | tf_op jit(solution)/shard_map/ppermute | solution.py:491
